TPU v7x, 32 devices: a whole 2x2x4 slice. The times are simulated.
32 devices in a mesh: blk: 16 (over z, x, core), rep: 2 (over y).
Axes of the slice: x: 2, y: 2, z: 4, core: 2. Of those that a mesh axis runs over, the one named last changes fastest.
Arguments:
- captions: bfloat16 [6144, 768], P(('blk', 'rep')), may hold values from -512 to 512
- images: bfloat16 [6144, 768], P(('blk', 'rep')), may hold values from -512 to 512
- positives: int32 [6144], P(('blk', 'rep')), may hold values from 0 to 6143, each once
- valid: int32 [6144], P(('blk', 'rep')), may hold values from 0 to 1, as said below
Outputs:
- caption_loss: float32 [6144], P(('blk', 'rep'))
- image_loss: float32 [6144], P(('blk', 'rep'))
- loss: float32 [], replicated
Inputs may be any that keep to these rules, and one draw needn't show every extreme that they name: `positives`: each image row is the positive of exactly one caption; a program may pack several of these indices into one sent element. `valid`: the last image row is always real; a program may pack several of these flags into one sent element.
All inputs are finite; a program needn't handle non-finite values.
Results may differ from a plain program's by a relative error of at most 0.0003.
Values may be sent and summed in bfloat16 or wider, within the bound.
A program may use at most 128 MiB of HBM per device.

v0:
```python
import functools

import jax
import jax.numpy as jnp
from jax import lax
from jax.experimental import pallas as pl
from jax.experimental.pallas import tpu as pltpu
from jax.sharding import PartitionSpec as P

very_low = -1e30
floor = -1e29
PIECES = 2


def grid_of(blk, rep):
    chips = (blk // 2) * rep
    planes = 1
    while (planes * 2) ** 2 <= chips and (blk // 2) % (planes * 2) == 0:
        planes *= 2
    return planes, blk // 2 // planes


def mod(a, b):
    return a & (b - 1) if b & (b - 1) == 0 else lax.rem(a, b)


def div(a, b):
    return a >> (b.bit_length() - 1) if b & (b - 1) == 0 else lax.div(a, b)


def kernel(
    blk, rep, cap_ref, img_ref, pos_ref, val_ref, closs_ref, iloss_ref, loss_ref,
    caps, imgs, posb, vbuf, rowsend, rowrecv, colsend, colrecv, part, colacc,
    loc_sem, up_sem, down_sem, cap_sem, pos_send, pos_recv, val_send, val_recv, plane_send, plane_recv,
    own_send, relay_send, corner_send, img_sem, row_send, row_recv, col_send, col_recv, part_send, part_recv,
):
    U, V = grid_of(blk, rep)
    N = blk * rep
    G = N // U
    n = cap_ref.shape[0]
    ph = n // PIECES
    b, r = lax.axis_index("blk"), lax.axis_index("rep")
    core = mod(b, 2)
    u = div(b, 2 * V)
    v = mod(div(b, 2), V)
    me = b * rep + r
    g = mod(me, G)

    def member(uu, gg):
        return uu * G + gg

    def remote(src, dst, ss, rs, to):
        return pltpu.make_async_remote_copy(
            src_ref=src, dst_ref=dst, send_sem=ss, recv_sem=rs, device_id=to,
            device_id_type=pl.DeviceIdType.LOGICAL,
        )

    barrier = pltpu.get_barrier_semaphore()

    near = [member(u, mod(g + k, G)) for k in range(1, G)]
    near += [member(mod(u + k, U), g) for k in range(1, U)]
    for to in near:
        pl.semaphore_signal(
            barrier, inc=1, device_id=to, device_id_type=pl.DeviceIdType.LOGICAL
        )
    pl.semaphore_wait(barrier, len(near))

    def cap_copy(slot, p, up):
        rows = pl.ds(p * ph, ph)
        to = member(u + 1 if up else u - 1, g)
        return remote(
            caps.at[slot, rows], caps.at[slot, rows],
            (up_sem if up else down_sem).at[slot * PIECES + p], cap_sem.at[slot * PIECES + p], to,
        )

    def own_cap_copy(p, up):
        rows = pl.ds(p * ph, ph)
        to = member(u + 1 if up else u - 1, g)
        return remote(
            cap_ref.at[rows], caps.at[u, rows],
            (up_sem if up else down_sem).at[u * PIECES + p], cap_sem.at[u * PIECES + p], to,
        )

    def pos_copy(k):
        return remote(
            pos_ref, posb.at[u], pos_send.at[k], pos_recv.at[u], member(mod(u + k, U), g)
        )

    for k in range(1, U):
        pos_copy(k).start()

    def val_copy(k):
        return remote(
            val_ref, vbuf.at[me], val_send.at[k], val_recv.at[g], member(u, mod(g + k, G))
        )

    for k in range(1, G):
        val_copy(k).start()

    def plane_copy(k):
        rows = pl.ds(u * G, G)
        return remote(
            vbuf.at[rows], vbuf.at[rows], plane_send.at[k], plane_recv.at[u],
            member(mod(u + k, U), g),
        )

    for p in range(PIECES):
        @pl.when(u < U - 1)
        def _():
            own_cap_copy(p, True).start()

        @pl.when(u > 0)
        def _():
            own_cap_copy(p, False).start()

    def same_core(k):
        vv, rr = mod(v + k // rep, V), mod(r + k % rep, rep)
        return (vv * 2 + core) * rep + rr

    partner = (v * 2 + 1 - core) * rep + r
    M = V * rep

    def own_img_copy(k):
        to = partner if k == 0 else same_core(k)
        return remote(img_ref, imgs.at[g], own_send.at[k], img_sem.at[g], member(u, to))

    def relay_copy(k):
        slot = same_core(k)
        return remote(
            imgs.at[slot], imgs.at[slot], relay_send.at[k], img_sem.at[slot], member(u, partner)
        )

    sides = [k for k in range(1, M) if k < rep or k % rep == 0]
    corners = [k for k in range(1, M) if k not in sides]

    def corner_copy(k, half):
        if half == 0:
            slot, to = same_core(k - k % rep), same_core(k % rep)
        else:
            slot, to = same_core(k % rep), same_core(k - k % rep)
        rows = pl.ds(half * (n // 2), n // 2)
        return remote(
            imgs.at[slot, rows], imgs.at[slot, rows], corner_send.at[half * M + k],
            img_sem.at[half * G + slot], member(u, to),
        )

    def corner_arrival(k, half):
        slot = same_core(k)
        rows = pl.ds(half * (n // 2), n // 2)
        return remote(
            imgs.at[slot, rows], imgs.at[slot, rows], corner_send.at[half * M + k],
            img_sem.at[half * G + slot], member(u, slot),
        )

    for k in sides + [0]:
        own_img_copy(k).start()

    cap_local = pltpu.make_async_copy(cap_ref, caps.at[u], loc_sem.at[0])
    img_local = pltpu.make_async_copy(img_ref, imgs.at[g], loc_sem.at[1])
    cap_local.start()
    img_local.start()
    posb[u] = pos_ref[...]
    vbuf[me] = val_ref[...]

    def pass_on(distance):
        for p in range(PIECES):
            @pl.when(u - distance >= 0)
            def _():
                copy = cap_copy(u - distance, p, True)
                copy.wait_recv()

                @pl.when(u < U - 1)
                def _():
                    copy.start()

            @pl.when(u + distance < U)
            def _():
                copy = cap_copy(u + distance, p, False)
                copy.wait_recv()

                @pl.when(u > 0)
                def _():
                    copy.start()

    for k in range(1, G):
        slot = mod(g + k, G)
        remote(
            val_ref, vbuf.at[u * G + slot], val_send.at[k], val_recv.at[slot], member(u, slot)
        ).wait_recv()
    for k in range(1, U):
        plane_copy(k).start()
    if U > 2:
        pass_on(1)
    for k in sides:
        copy = relay_copy(k)
        copy.wait_recv()
        for c in corners:
            if k == c - c % rep:
                corner_copy(c, 0).start()
            if k == c % rep:
                corner_copy(c, 1).start()
        copy.start()
    for d in range(2, U - 1):
        pass_on(d)
    for k in corners:
        corner_arrival(k, 0).wait_recv()
        corner_arrival(k, 1).wait_recv()
        relay_copy(k).start()
    for k in range(1, U):
        slot = mod(u + k, U)
        rows = pl.ds(slot * G, G)
        remote(
            vbuf.at[rows], vbuf.at[rows], plane_send.at[k], plane_recv.at[slot], member(slot, g)
        ).wait_recv()
    for k in range(1, U):
        slot = mod(u + k, U)
        remote(
            pos_ref, posb.at[slot], pos_send.at[k], pos_recv.at[slot], member(slot, g)
        ).wait_recv()

    eye = lax.broadcasted_iota(jnp.int32, (n, n), 0) == lax.broadcasted_iota(jnp.int32, (n, n), 1)

    def to_column(row):
        return jnp.sum(jnp.where(eye, row, 0.0), axis=1, keepdims=True)

    def to_row(column):
        return jnp.sum(jnp.where(eye, column, 0.0), axis=0, keepdims=True)

    flags = vbuf[:, 0, :].astype(jnp.float32)
    image_total = jnp.sum(jnp.sum(flags, axis=1, keepdims=True), axis=0, keepdims=True)
    starts = lax.broadcasted_iota(jnp.int32, (n, N), 1) * n
    lanes = lax.broadcasted_iota(jnp.int32, (n, n), 1)

    def caption_state(slot):
        target = to_column(posb[slot].astype(jnp.float32)).astype(jnp.int32)
        inside = (target >= starts) & (target < starts + n)
        picked = jnp.dot(
            jnp.where(inside, 1.0, 0.0).astype(jnp.bfloat16), flags.astype(jnp.bfloat16),
            preferred_element_type=jnp.float32,
        )
        start = jnp.sum(jnp.where(inside, starts, 0).astype(jnp.float32), axis=1, keepdims=True)
        low = target - start.astype(jnp.int32)
        ok = jnp.sum(jnp.where(lanes == low, picked, 0.0), axis=1, keepdims=True)
        return target, ok

    image_ok = jnp.concatenate(
        [vbuf[u * G + s].astype(jnp.float32) for s in range(G)], axis=1
    )
    image_ids = u * (G * n) + lax.broadcasted_iota(jnp.int32, (1, G * n), 1)
    colacc[0:1, :] = jnp.full((1, G * n), floor, jnp.float32)
    colacc[1:3, :] = jnp.zeros((2, G * n), jnp.float32)

    img_local.wait()
    cap_local.wait()
    for k in range(M):
        slot = partner if k == 0 else same_core(k) + (1 - 2 * core) * rep
        remote(
            img_ref, imgs.at[slot], own_send.at[0], img_sem.at[slot], member(u, partner)
        ).wait_recv()

    small = jnp.minimum(u, U - 1 - u)
    side = jnp.where(u < U - 1 - u, 1, -1)

    def slot_at(k):
        near = jnp.where(mod(k, 2) == 1, u - div(k + 1, 2), u + div(k + 1, 2))
        return jnp.where(k <= 2 * small, near, u + side * (k - small))

    def row_copy(slot):
        return remote(
            rowsend.at[slot], rowrecv.at[u], row_send.at[slot], row_recv.at[u], member(slot, g)
        )

    @pl.loop(0, U)
    def _(k):
        slot = slot_at(k)

        @pl.when((slot - u == U - 1) | (u - slot == U - 1))
        def _():
            for p in range(PIECES):
                rows = pl.ds(p * ph, ph)
                remote(
                    caps.at[slot, rows], caps.at[slot, rows], up_sem.at[slot * PIECES + p],
                    cap_sem.at[slot * PIECES + p], member(slot, g),
                ).wait_recv()

        target, ok = caption_state(slot)
        scores = lax.dot_general(
            caps[slot], imgs[...].reshape(G * n, imgs.shape[2]), (((1,), (1,)), ((), ())),
            preferred_element_type=jnp.float32,
        )
        usable = jnp.where(image_ok > 0, scores, very_low)
        row_peak = jnp.maximum(jnp.max(usable, axis=1, keepdims=True), floor)
        row_total = jnp.sum(jnp.exp(usable - row_peak), axis=1, keepdims=True)
        picked = jnp.where(target == image_ids, scores, 0.0)
        row_match = jnp.sum(picked, axis=1, keepdims=True)
        rowsend[slot, 0:1, :] = to_row(row_peak)
        rowsend[slot, 1:2, :] = to_row(row_total)
        rowsend[slot, 2:3, :] = to_row(row_match)

        @pl.when(slot != u)
        def _():
            row_copy(slot).start()

        live = jnp.where(ok > 0, scores, very_low)
        old_peak = colacc[0:1, :]
        peak = jnp.maximum(jnp.max(live, axis=0, keepdims=True), old_peak)
        total = jnp.sum(jnp.exp(live - peak), axis=0, keepdims=True)
        colacc[1:2, :] = colacc[1:2, :] * jnp.exp(old_peak - peak) + total
        colacc[0:1, :] = peak
        colacc[2:3, :] = colacc[2:3, :] + jnp.sum(picked, axis=0, keepdims=True)

    for s in range(G):
        colsend[s, 0:3, :] = colacc[0:3, s * n : (s + 1) * n]

    def col_copy(k):
        slot = mod(g + k, G)
        return remote(
            colsend.at[slot], colrecv.at[g], col_send.at[k], col_recv.at[g], member(u, slot)
        )

    for k in range(1, G):
        col_copy(k).start()

    rowrecv[u] = rowsend[u]
    colrecv[g] = colsend[g]
    own_target, own_caption_ok = caption_state(u)
    caption_ok = to_row(own_caption_ok)

    def joined(parts, count):
        peak = parts[0, 0:1, :]
        for s in range(1, count):
            peak = jnp.maximum(peak, parts[s, 0:1, :])
        total = jnp.zeros_like(peak)
        match = jnp.zeros_like(peak)
        for s in range(count):
            total += parts[s, 1:2, :] * jnp.exp(parts[s, 0:1, :] - peak)
            match += parts[s, 2:3, :]
        return peak + jnp.log(total) - match

    for k in range(1, U):
        slot = mod(u + k, U)
        remote(
            rowsend.at[slot], rowrecv.at[slot], row_send.at[slot], row_recv.at[slot],
            member(slot, g),
        ).wait_recv()
    caption_loss = caption_ok * joined(rowrecv, U)
    closs_ref[...] = caption_loss
    for k in range(1, G):
        slot = mod(g + k, G)
        remote(
            colsend.at[slot], colrecv.at[slot], col_send.at[k], col_recv.at[slot],
            member(u, slot),
        ).wait_recv()
    image_loss = val_ref[...].astype(jnp.float32) * joined(colrecv, G)
    iloss_ref[...] = image_loss
    own_sum = jnp.sum(caption_loss + image_loss, axis=1, keepdims=True)
    part[me] = jnp.broadcast_to(own_sum, (1, 128))

    def part_copy(k):
        return remote(
            part.at[me], part.at[me], part_send.at[k], part_recv.at[me], mod(me + k, N)
        )

    @pl.loop(1, N)
    def _(k):
        part_copy(k).start()

    for d in range(U - 1):
        for p in range(PIECES):
            @pl.when((u - d >= 0) & (u < U - 1))
            def _():
                cap_copy(u - d, p, True).wait_send()

            @pl.when((u + d < U) & (u > 0))
            def _():
                cap_copy(u + d, p, False).wait_send()

    for k in [0] + sides:
        own_img_copy(k).wait_send()
    for k in range(1, M):
        relay_copy(k).wait_send()
    for k in corners:
        corner_copy(k, 0).wait_send()
        corner_copy(k, 1).wait_send()
    for k in range(1, U):
        pos_copy(k).wait_send()
        row_copy(mod(u + k, U)).wait_send()
    for k in range(1, G):
        col_copy(k).wait_send()

    for k in range(1, G):
        val_copy(k).wait_send()
    for k in range(1, U):
        plane_copy(k).wait_send()

    @pl.loop(1, N)
    def _(k):
        slot = mod(me + k, N)
        remote(
            part.at[slot], part.at[slot], part_send.at[k], part_recv.at[slot], slot
        ).wait_recv()

    whole = jnp.sum(part[:, 0, :], axis=0, keepdims=True)
    loss_ref[...] = whole[:, 0:1] / (2.0 * image_total)

    @pl.loop(1, N)
    def _(k):
        part_copy(k).wait_send()


def local(blk, rep, captions, images, positives, valid):
    n, width = captions.shape
    U, V = grid_of(blk, rep)
    N = blk * rep
    G = N // U
    f32, i32 = jnp.float32, jnp.int32
    dma = lambda count: pltpu.SemaphoreType.DMA((count,))
    vmem = pl.BlockSpec(memory_space=pltpu.VMEM)
    caption_loss, image_loss, loss = pl.pallas_call(
        functools.partial(kernel, blk, rep),
        out_shape=(
            jax.ShapeDtypeStruct((1, n), f32),
            jax.ShapeDtypeStruct((1, n), f32),
            jax.ShapeDtypeStruct((1, 1), f32),
        ),
        in_specs=[vmem] * 4,
        out_specs=(vmem,) * 3,
        scratch_shapes=[
            pltpu.VMEM((U, n, width), captions.dtype),
            pltpu.VMEM((G, n, width), images.dtype),
            pltpu.VMEM((U, 1, n), i32),
            pltpu.VMEM((N, 1, n), i32),
            pltpu.VMEM((U, 8, n), f32),
            pltpu.VMEM((U, 8, n), f32),
            pltpu.VMEM((G, 8, n), f32),
            pltpu.VMEM((G, 8, n), f32),
            pltpu.VMEM((N, 1, 128), f32),
            pltpu.VMEM((8, G * n), f32),
            dma(2), dma(U * PIECES), dma(U * PIECES), dma(U * PIECES),
            dma(U), dma(U), dma(G), dma(G), dma(U), dma(U),
            dma(V * rep), dma(V * rep), dma(2 * V * rep), dma(2 * G),
            dma(U), dma(U), dma(G), dma(G), dma(N), dma(N),
        ],
        compiler_params=pltpu.CompilerParams(collective_id=0, has_side_effects=True),
    )(captions, images, positives.reshape(1, n), valid.reshape(1, n))
    return caption_loss.reshape(n), image_loss.reshape(n), loss.reshape(())


def solution(mesh):
    placed = (
        P(("blk", "rep"), None),
        P(("blk", "rep"), None),
        P(("blk", "rep")),
        P(("blk", "rep")),
    )
    return jax.shard_map(
        functools.partial(local, mesh.shape["blk"], mesh.shape["rep"]),
        mesh=mesh,
        in_specs=placed,
        out_specs=(P(("blk", "rep")), P(("blk", "rep")), P()),
        check_vma=False,
    )
```

profile of v0, /device:TPU:0, one launch (start us, length us, event | category | flops | bytes accessed | tf_op | source)
XLA Modules:
  0.0 43.7 jit_solution(9273966478487488997)
XLA Ops:
  0.6 39.4 %shard_map.67 = (f32[1,192]{1,0:T(1,128)}, f32[1,192]{1,0:T(1,128)}, f32[1,1]{1,0:T(1,128)}) custom-call(bf16[192,768]{1,0:T(8,128)(2,1)} %cap_ref.1, bf16[192,768]{1,0:T(8,128)(2,1)} %img_ref.1, s32[1,192]{1,0:T(1,128)} %bitcast.5, s32[1,192]{1,0:T(1,128)} %bitcast.6), custom_call_target="tpu_custom_call" | custom-call | tf_op jit(solution)/shard_map/pallas_call | solution.py:419
  40.1 0.0 copy-start.1
  40.1 0.7 %copy-done.1 = f32[1,192]{1,0:T(1,128)S(1)} copy-done((f32[1,192]{1,0:T(1,128)S(1)}, f32[1,192]{1,0:T(1,128)}, u32[]{:S(2)}) %copy-start.1) | copy-done | bytes 792
  40.7 0.0 copy-start
  40.7 0.6 %copy.10 = f32[192]{0:T(256)} copy(f32[192]{0:T(256)S(1)} %bitcast.8) | data formatting | bytes 1536
  41.3 0.1 copy-done
  41.4 0.6 %copy.11 = f32[192]{0:T(256)} copy(f32[192]{0:T(256)S(1)} %bitcast.7) | data formatting | bytes 1536
Async XLA Ops:
  40.1 0.7 %copy-start.1 = (f32[1,192]{1,0:T(1,128)S(1)}, f32[1,192]{1,0:T(1,128)}, u32[]{:S(2)}) copy-start(f32[1,192]{1,0:T(1,128)} %get-tuple-element.6) | copy-start | bytes 2308
  40.7 0.6 %copy-start = (f32[1,192]{1,0:T(1,128)S(1)}, f32[1,192]{1,0:T(1,128)}, u32[]{:S(2)}) copy-start(f32[1,192]{1,0:T(1,128)} %get-tuple-element.7) | copy-start | bytes 2308
where the time goes:
time: 43.9 us; the launch traced here: 43.7 us
  Pallas kernels  39.4 us (90%)
  between operations  2.4 us (5%)
  local copies, waits for them, and re-layouts  1.86 us (4%)
    pallas_call x1, Pallas kernels, local(): pl.pallas_call(functools.partial(kernel, blk, rep), out_shape=(jax.ShapeD...  39.4 us
    unnamed x6, local copies, waits for them, and re-layouts  1.86 us

commit v1 on v0

v1 whole, which is shorter than its diff:
```python
import functools

import jax
import jax.numpy as jnp
from jax import lax
from jax.experimental import pallas as pl
from jax.experimental.pallas import tpu as pltpu
from jax.sharding import PartitionSpec as P

very_low = -1e30
floor = -1e29
IMAGE_PIECES = 4
CAPTION_PIECES = 4
LAST_PIECES = 2


def grid_of(blk, rep):
    chips = (blk // 2) * rep
    planes = 1
    while (planes * 2) ** 2 <= chips and (blk // 2) % (planes * 2) == 0:
        planes *= 2
    return planes, blk // 2 // planes


def mod(a, b):
    return a & (b - 1) if b & (b - 1) == 0 else lax.rem(a, b)


def div(a, b):
    return a >> (b.bit_length() - 1) if b & (b - 1) == 0 else lax.div(a, b)


def kernel(
    blk, rep, cap_ref, img_ref, pos_ref, val_ref, closs_ref, iloss_ref, loss_ref,
    mine, caps, imgs, vbuf, image_ok, image_ids, target, caption_ok, own_ok,
    row_peak, row_total, row_match, colacc, rowsend, rowrecv, colsend, colrecv, part, closs, iloss,
    loc_sem, out_sem, img_recv, imgz_send, imgv_send, imgd_send, cap_recv, capz_send, capr_send,
    val_send, val_recv, plane_send, plane_recv,
    row_send, row_recv, col_send, col_recv, part_send, part_recv,
):
    U, V = grid_of(blk, rep)
    N = blk * rep
    G = N // U
    H = U // 2
    B = V * 2
    n, width = cap_ref.shape
    C = B * n
    b, r = lax.axis_index("blk"), lax.axis_index("rep")
    c = mod(b, 2)
    u = div(b, 2 * V)
    v = mod(div(b, 2), V)
    me = b * rep + r
    g = mod(me, G)
    half, h = div(u, H), mod(u, H)
    near = jnp.where(u > 2 * h, 1, 0)
    far = 1 - near
    keeps_own = div(u, 2) == h

    def member(uu, vv, cc, rr):
        return ((uu * V + vv) * 2 + cc) * rep + rr

    def remote(src, dst, ss, rs, to):
        return pltpu.make_async_remote_copy(
            src_ref=src, dst_ref=dst, send_sem=ss, recv_sem=rs, device_id=to,
            device_id_type=pl.DeviceIdType.LOGICAL,
        )

    barrier = pltpu.get_barrier_semaphore()
    others = [u * G + mod(g + k, G) for k in range(1, G)]
    others += [mod(u + k, U) * G + g for k in range(1, U)]
    for to in others:
        pl.semaphore_signal(
            barrier, inc=1, device_id=to, device_id_type=pl.DeviceIdType.LOGICAL
        )

    load_val = pltpu.make_async_copy(val_ref, vbuf.at[me, 0], loc_sem.at[0])
    load_pos = pltpu.make_async_copy(pos_ref, vbuf.at[me, 1], loc_sem.at[1])
    load_img = pltpu.make_async_copy(img_ref, imgs.at[h, v, c], loc_sem.at[2])
    load_cap = pltpu.make_async_copy(cap_ref, mine, loc_sem.at[3])
    keep_cap = pltpu.make_async_copy(cap_ref, caps.at[mod(u, 2), r], loc_sem.at[4])
    load_val.start()
    load_pos.start()
    load_img.start()
    load_cap.start()

    @pl.when(keeps_own)
    def _():
        keep_cap.start()

    load_val.wait()
    load_pos.wait()
    load_img.wait()
    load_cap.wait()

    @pl.when(keeps_own)
    def _():
        keep_cap.wait()

    pl.semaphore_wait(barrier, len(others))

    def image_rows(k):
        return pl.ds(k * (n // IMAGE_PIECES), n // IMAGE_PIECES)

    def caption_rows(k):
        return pl.ds(k * (n // CAPTION_PIECES), n // CAPTION_PIECES)

    def img_copy(i, vv, cc, k, ss, to):
        block = imgs.at[i, vv, cc, image_rows(k)]
        return remote(block, block, ss, img_recv.at[((i * V + vv) * 2 + cc) * IMAGE_PIECES + k], to)

    def img_along(d, k):
        to = member(half * H + mod(h + d, H), v, c, r)
        return img_copy(h, v, c, k, imgz_send.at[d * IMAGE_PIECES + k], to)

    def img_across(i, d, k):
        to = member(u, mod(v + d, V), c, r)
        return img_copy(i, v, c, k, imgv_send.at[(i * V + d) * IMAGE_PIECES + k], to)

    def img_beside(i, vv, k):
        to = member(u, v, 1 - c, r)
        return img_copy(i, vv, c, k, imgd_send.at[(i * V + vv) * IMAGE_PIECES + k], to)

    def img_arrival(i, vv, cc, k):
        return img_copy(i, vv, cc, k, imgd_send.at[0], member(u, v, 1 - c, r))

    def cap_along(t, k):
        rows = caption_rows(k)
        return remote(
            mine.at[rows], caps.at[mod(u, 2), r, rows], capz_send.at[t * CAPTION_PIECES + k],
            cap_recv.at[(mod(u, 2) * rep + r) * CAPTION_PIECES + k],
            member(t * H + div(u, 2), v, c, r),
        )

    def cap_across(q, d, k):
        block = caps.at[q, r, caption_rows(k)]
        return remote(
            block, block, capr_send.at[(q * rep + d) * CAPTION_PIECES + k],
            cap_recv.at[(q * rep + r) * CAPTION_PIECES + k], member(u, v, c, mod(r + d, rep)),
        )

    def cap_arrival(q, rr, k):
        block = caps.at[q, rr, caption_rows(k)]
        return remote(
            block, block, capr_send.at[0], cap_recv.at[(q * rep + rr) * CAPTION_PIECES + k],
            member(u, v, 1 - c, r),
        )

    def val_copy(k):
        return remote(
            vbuf.at[me], vbuf.at[me], val_send.at[k], val_recv.at[g], u * G + mod(g + k, G)
        )

    def plane_copy(k):
        rows = pl.ds(u * G, G)
        return remote(
            vbuf.at[rows], vbuf.at[rows], plane_send.at[k], plane_recv.at[u],
            mod(u + k, U) * G + g,
        )

    for k in range(1, G):
        val_copy(k).start()
    for k in range(IMAGE_PIECES):
        for d in range(1, H):
            img_along(d, k).start()
        for d in range(1, V):
            img_across(h, d, k).start()
        img_beside(h, v, k).start()
    for k in range(CAPTION_PIECES):
        for t in range(2):
            @pl.when(t * H + div(u, 2) != u)
            def _():
                cap_along(t, k).start()

        @pl.when(keeps_own)
        def _():
            for d in range(1, rep):
                cap_across(mod(u, 2), d, k).start()

    for k in range(1, G):
        slot = mod(g + k, G)
        remote(
            vbuf.at[me], vbuf.at[u * G + slot], val_send.at[k], val_recv.at[slot], u * G + slot
        ).wait_recv()
    for k in range(1, U):
        plane_copy(k).start()

    def relay_images(k):
        for d in range(1, H):
            i = mod(h + d, H)
            img_arrival(i, v, c, k).wait_recv()
            for dv in range(1, V):
                img_across(i, dv, k).start()
            img_beside(i, v, k).start()

    def relay_beside(i, k):
        for dv in range(1, V):
            vv = mod(v + dv, V)
            img_arrival(i, vv, c, k).wait_recv()
            img_beside(i, vv, k).start()

    def relay_captions(q, k):
        cap_arrival(q, r, k).wait_recv()
        for d in range(1, rep):
            cap_across(q, d, k).start()

    for k in range(IMAGE_PIECES):
        relay_images(k)
        relay_beside(h, k)
        if k < CAPTION_PIECES:
            @pl.when(jnp.logical_not(keeps_own))
            def _():
                relay_captions(near, k)

    for k in range(IMAGE_PIECES, CAPTION_PIECES):
        @pl.when(jnp.logical_not(keeps_own))
        def _():
            relay_captions(near, k)

    for k in range(1, U):
        slot = mod(u + k, U)
        rows = pl.ds(slot * G, G)
        remote(
            vbuf.at[rows], vbuf.at[rows], plane_send.at[k], plane_recv.at[slot], slot * G + g
        ).wait_recv()

    eye = lax.broadcasted_iota(jnp.int32, (n, n), 0) == lax.broadcasted_iota(jnp.int32, (n, n), 1)

    def to_column(row):
        return jnp.sum(jnp.where(eye, row, 0.0), axis=1, keepdims=True)

    def to_row(column):
        return jnp.sum(jnp.where(eye, column, 0.0), axis=0, keepdims=True)

    flags = vbuf[:, 0, 0, :].astype(jnp.float32)
    image_total = jnp.sum(jnp.sum(flags, axis=1, keepdims=True), axis=0, keepdims=True)
    starts = lax.broadcasted_iota(jnp.int32, (n, N), 1) * n
    lanes = lax.broadcasted_iota(jnp.int32, (n, n), 1)

    def caption_state(row):
        aim = to_column(row.astype(jnp.float32)).astype(jnp.int32)
        inside = (aim >= starts) & (aim < starts + n)
        picked = jnp.dot(
            jnp.where(inside, 1.0, 0.0).astype(jnp.bfloat16), flags.astype(jnp.bfloat16),
            preferred_element_type=jnp.float32,
        )
        start = jnp.sum(jnp.where(inside, starts, 0).astype(jnp.float32), axis=1, keepdims=True)
        low = aim - start.astype(jnp.int32)
        ok = jnp.sum(jnp.where(lanes == low, picked, 0.0), axis=1, keepdims=True)
        return aim, ok

    @pl.loop(0, 2 * rep)
    def _(s):
        aim, ok = caption_state(vbuf[member(2 * h + div(s, rep), v, c, mod(s, rep)), 1])
        target[s] = aim
        caption_ok[s] = ok

    own_ok[...] = to_row(caption_state(vbuf[me, 1])[1])
    for i in range(H):
        base = (half * H + i) * G
        for s in range(B):
            at = base + s * rep + r
            cols = slice(s * n, (s + 1) * n)
            image_ok[i, :, cols] = vbuf[at, 0].astype(jnp.float32)
            image_ids[i, :, cols] = at * n + lax.broadcasted_iota(jnp.int32, (1, n), 1)
    colacc[:, 0:1, :] = jnp.full((H, 1, C), floor, jnp.float32)
    colacc[:, 1:3, :] = jnp.zeros((H, 2, C), jnp.float32)
    row_peak[...] = jnp.full(row_peak.shape, floor, jnp.float32)
    row_total[...] = jnp.zeros(row_total.shape, jnp.float32)
    row_match[...] = jnp.zeros(row_match.shape, jnp.float32)

    def score(q, rr, i, start, rows):
        s = q * rep + rr
        part_rows = pl.ds(start, rows)
        scores = lax.dot_general(
            caps[q, rr, part_rows], imgs[i].reshape(C, width), (((1,), (1,)), ((), ())),
            preferred_element_type=jnp.float32,
        )
        usable = jnp.where(image_ok[i] > 0, scores, very_low)
        old = row_peak[s, part_rows]
        peak = jnp.maximum(jnp.max(usable, axis=1, keepdims=True), old)
        total = jnp.sum(jnp.exp(usable - peak), axis=1, keepdims=True)
        row_total[s, part_rows] = row_total[s, part_rows] * jnp.exp(old - peak) + total
        row_peak[s, part_rows] = peak
        picked = jnp.where(target[s, part_rows] == image_ids[i], scores, 0.0)
        row_match[s, part_rows] = row_match[s, part_rows] + jnp.sum(picked, axis=1, keepdims=True)
        live = jnp.where(caption_ok[s, part_rows] > 0, scores, very_low)
        old_peak = colacc[i, 0:1, :]
        peak = jnp.maximum(jnp.max(live, axis=0, keepdims=True), old_peak)
        total = jnp.sum(jnp.exp(live - peak), axis=0, keepdims=True)
        colacc[i, 1:2, :] = colacc[i, 1:2, :] * jnp.exp(old_peak - peak) + total
        colacc[i, 0:1, :] = peak
        colacc[i, 2:3, :] = colacc[i, 2:3, :] + jnp.sum(picked, axis=0, keepdims=True)

    def wait_beside(i):
        for vv in range(V):
            for k in range(IMAGE_PIECES):
                img_arrival(i, vv, 1 - c, k).wait_recv()

    wait_beside(h)

    @pl.loop(0, rep)
    def _(d):
        rr = mod(r + d, rep)

        @pl.when(d > 0)
        def _():
            for k in range(CAPTION_PIECES):
                cap_arrival(near, rr, k).wait_recv()
        score(near, rr, h, 0, n)

    for k in range(CAPTION_PIECES):
        relay_captions(far, k)
        if k < IMAGE_PIECES:
            for d in range(1, H):
                relay_beside(mod(h + d, H), k)
    for k in range(CAPTION_PIECES, IMAGE_PIECES):
        for d in range(1, H):
            relay_beside(mod(h + d, H), k)

    @pl.loop(0, 1 + (H - 1) * (rep + 1))
    def _(t):
        first = t == 0
        e = jnp.maximum(t - 1, 0)
        i = mod(h + jnp.where(first, 0, 1 + div(e, rep + 1)), H)
        d = jnp.where(first, rep, lax.rem(e, rep + 1))

        @pl.when(jnp.logical_not(first) & (d == 0))
        def _():
            wait_beside(i)
        score(jnp.where(d == rep, far, near), mod(r + d, rep), i, 0, n)

    def row_copy(s):
        q, rr = div(s, rep), mod(s, rep)
        return remote(
            rowsend.at[s], rowrecv.at[half * rep + r], row_send.at[s],
            row_recv.at[half * rep + r], member(2 * h + q, v, c, rr),
        )

    def send_rows(s):
        rowsend[s, 0:1, :] = to_row(row_peak[s])
        rowsend[s, 1:2, :] = to_row(row_total[s])
        rowsend[s, 2:3, :] = to_row(row_match[s])

        @pl.when((2 * h + div(s, rep) != u) | (mod(s, rep) != r))
        def _():
            row_copy(s).start()

        @pl.when((2 * h + div(s, rep) == u) & (mod(s, rep) == r))
        def _():
            rowrecv[half * rep + r] = rowsend[s]

    @pl.loop(0, rep + 1)
    def _(d):
        send_rows(jnp.where(d == rep, far, near) * rep + mod(r + d, rep))

    @pl.loop(1, rep)
    def _(d):
        rr = mod(r + d, rep)

        @pl.loop(0, LAST_PIECES)
        def _(k):
            for j in range(CAPTION_PIECES // LAST_PIECES):
                cap_arrival(far, rr, k * (CAPTION_PIECES // LAST_PIECES) + j).wait_recv()

            @pl.loop(0, H)
            def _(e):
                score(far, rr, mod(h + e, H), k * (n // LAST_PIECES), n // LAST_PIECES)
        send_rows(far * rep + rr)

    for i in range(H):
        for s in range(B):
            colsend[i * B + s, 0:3, :] = colacc[i, 0:3, s * n : (s + 1) * n]

    own_at = h * B + v * 2 + c

    def col_copy(k):
        slot = mod(own_at + k, H * B)
        i, s = div(slot, B), mod(slot, B)
        return remote(
            colsend.at[slot], colrecv.at[own_at], col_send.at[k], col_recv.at[own_at],
            (half * H + i) * G + s * rep + r,
        )

    for k in range(1, H * B):
        col_copy(k).start()
    colrecv[own_at] = colsend[own_at]

    def joined(parts, count):
        peak = parts[0, 0:1, :]
        for s in range(1, count):
            peak = jnp.maximum(peak, parts[s, 0:1, :])
        total = jnp.zeros_like(peak)
        match = jnp.zeros_like(peak)
        for s in range(count):
            total += parts[s, 1:2, :] * jnp.exp(parts[s, 0:1, :] - peak)
            match += parts[s, 2:3, :]
        return peak + jnp.log(total) - match

    for t in range(2):
        for rr in range(rep):
            @pl.when((t * H + div(u, 2) != u) | (rr != r))
            def _():
                remote(
                    rowsend.at[0], rowrecv.at[t * rep + rr], row_send.at[0],
                    row_recv.at[t * rep + rr], member(u, v, 1 - c, r),
                ).wait_recv()
    caption_loss = own_ok[...] * joined(rowrecv, 2 * rep)
    closs[...] = caption_loss
    put_caption = pltpu.make_async_copy(closs, closs_ref, out_sem.at[0])
    put_caption.start()
    for k in range(1, H * B):
        slot = mod(own_at + k, H * B)
        remote(
            colsend.at[slot], colrecv.at[slot], col_send.at[k], col_recv.at[slot],
            member(u, v, 1 - c, r),
        ).wait_recv()
    image_loss = vbuf[me, 0].astype(jnp.float32) * joined(colrecv, H * B)
    iloss[...] = image_loss
    put_image = pltpu.make_async_copy(iloss, iloss_ref, out_sem.at[1])
    put_image.start()
    own_sum = jnp.sum(caption_loss + image_loss, axis=1, keepdims=True)
    part[me] = jnp.broadcast_to(own_sum, (1, 128))

    def part_copy(k):
        return remote(
            part.at[me], part.at[me], part_send.at[k], part_recv.at[me], mod(me + k, N)
        )

    @pl.loop(1, N)
    def _(k):
        part_copy(k).start()

    for k in range(1, G):
        val_copy(k).wait_send()
    for k in range(1, U):
        plane_copy(k).wait_send()
    for k in range(IMAGE_PIECES):
        for d in range(1, H):
            img_along(d, k).wait_send()
        for i in range(H):
            for d in range(1, V):
                img_across(i, d, k).wait_send()
            for vv in range(V):
                img_beside(i, vv, k).wait_send()
    for k in range(CAPTION_PIECES):
        for t in range(2):
            @pl.when(t * H + div(u, 2) != u)
            def _():
                cap_along(t, k).wait_send()
        for q in range(2):
            for d in range(1, rep):
                cap_across(q, d, k).wait_send()

    @pl.loop(0, 2 * rep)
    def _(s):
        @pl.when((2 * h + div(s, rep) != u) | (mod(s, rep) != r))
        def _():
            row_copy(s).wait_send()
    for k in range(1, H * B):
        col_copy(k).wait_send()
    put_caption.wait()
    put_image.wait()

    @pl.loop(1, N)
    def _(k):
        slot = mod(me + k, N)
        remote(
            part.at[slot], part.at[slot], part_send.at[k], part_recv.at[slot], slot
        ).wait_recv()

    whole = jnp.sum(part[:, 0, :], axis=0, keepdims=True)
    loss_ref[...] = whole[:, 0:1] / (2.0 * image_total)

    @pl.loop(1, N)
    def _(k):
        part_copy(k).wait_send()


def local(blk, rep, captions, images, positives, valid):
    n, width = captions.shape
    U, V = grid_of(blk, rep)
    N = blk * rep
    G = N // U
    H, B = U // 2, V * 2
    C = B * n
    f32, i32 = jnp.float32, jnp.int32
    dma = lambda count: pltpu.SemaphoreType.DMA((count,))
    vmem = pl.BlockSpec(memory_space=pltpu.VMEM)
    hbm = pl.BlockSpec(memory_space=pl.ANY)
    caption_loss, image_loss, loss = pl.pallas_call(
        functools.partial(kernel, blk, rep),
        out_shape=(
            jax.ShapeDtypeStruct((1, n), f32),
            jax.ShapeDtypeStruct((1, n), f32),
            jax.ShapeDtypeStruct((1, 1), f32),
        ),
        in_specs=[hbm] * 4,
        out_specs=(hbm, hbm, vmem),
        scratch_shapes=[
            pltpu.VMEM((n, width), captions.dtype),
            pltpu.VMEM((2, rep, n, width), captions.dtype),
            pltpu.VMEM((H, V, 2, n, width), images.dtype),
            pltpu.VMEM((N, 2, 1, n), i32),
            pltpu.VMEM((H, 1, C), f32),
            pltpu.VMEM((H, 1, C), i32),
            pltpu.VMEM((2 * rep, n, 1), i32),
            pltpu.VMEM((2 * rep, n, 1), f32),
            pltpu.VMEM((1, n), f32),
            pltpu.VMEM((2 * rep, n, 1), f32),
            pltpu.VMEM((2 * rep, n, 1), f32),
            pltpu.VMEM((2 * rep, n, 1), f32),
            pltpu.VMEM((H, 8, C), f32),
            pltpu.VMEM((2 * rep, 8, n), f32),
            pltpu.VMEM((2 * rep, 8, n), f32),
            pltpu.VMEM((H * B, 8, n), f32),
            pltpu.VMEM((H * B, 8, n), f32),
            pltpu.VMEM((N, 1, 128), f32),
            pltpu.VMEM((1, n), f32),
            pltpu.VMEM((1, n), f32),
            dma(5), dma(2),
            dma(H * B * IMAGE_PIECES), dma(H * IMAGE_PIECES), dma(H * V * IMAGE_PIECES),
            dma(H * V * IMAGE_PIECES),
            dma(2 * rep * CAPTION_PIECES), dma(2 * CAPTION_PIECES), dma(2 * rep * CAPTION_PIECES),
            dma(G), dma(G), dma(U), dma(U),
            dma(2 * rep), dma(2 * rep), dma(H * B), dma(H * B), dma(N), dma(N),
        ],
        compiler_params=pltpu.CompilerParams(collective_id=0, has_side_effects=True),
    )(captions, images, positives.reshape(1, n), valid.reshape(1, n))
    return caption_loss.reshape(n), image_loss.reshape(n), loss.reshape(())


def solution(mesh):
    placed = (
        P(("blk", "rep"), None),
        P(("blk", "rep"), None),
        P(("blk", "rep")),
        P(("blk", "rep")),
    )
    return jax.shard_map(
        functools.partial(local, mesh.shape["blk"], mesh.shape["rep"]),
        mesh=mesh,
        in_specs=placed,
        out_specs=(P(("blk", "rep")), P(("blk", "rep")), P()),
        check_vma=False,
    )
```

time: 43.9 us -> 49.7 us (1.13)
  Pallas kernels: 39.4 us -> 45.2 us
    pallas_call x1, Pallas kernels: 39.4 us -> 45.2 us  [local(): pl.pallas_call(functools.partial(kernel, blk, rep), out_shape=(jax.ShapeD...]
where the time goes in v1:
time: 49.7 us; the launch traced here: 49.5 us
  Pallas kernels  45.2 us (91%)
  between operations  2.4 us (5%)
  local copies, waits for them, and re-layouts  1.86 us (4%)
    pallas_call x1, Pallas kernels, local(): pl.pallas_call(functools.partial(kernel, blk, rep), out_shape=(jax.ShapeD...  45.2 us
    unnamed x6, local copies, waits for them, and re-layouts  1.86 us

profile of v1, /device:TPU:0, one launch (start us, length us, event | category | flops | bytes accessed | tf_op | source)
XLA Modules:
  0.0 49.5 jit_solution(1303610010221705428)
XLA Ops:
  0.6 45.2 %shard_map.67 = (f32[1,192]{1,0:T(1,128)}, f32[1,192]{1,0:T(1,128)}, f32[1,1]{1,0:T(1,128)}) custom-call(bf16[192,768]{1,0:T(8,128)(2,1)} %cap_ref.1, bf16[192,768]{1,0:T(8,128)(2,1)} %img_ref.1, s32[1,192]{1,0:T(1,128)} %bitcast.5, s32[1,192]{1,0:T(1,128)} %bitcast.6), custom_call_target="tpu_custom_call" | custom-call | tf_op jit(solution)/shard_map/pallas_call | solution.py:490
  45.9 0.0 copy-start.1
  45.9 0.7 %copy-done.1 = f32[1,192]{1,0:T(1,128)S(1)} copy-done((f32[1,192]{1,0:T(1,128)S(1)}, f32[1,192]{1,0:T(1,128)}, u32[]{:S(2)}) %copy-start.1) | copy-done | bytes 792
  46.5 0.0 copy-start
  46.5 0.6 %copy.10 = f32[192]{0:T(256)} copy(f32[192]{0:T(256)S(1)} %bitcast.8) | data formatting | bytes 1536
  47.1 0.1 copy-done
  47.2 0.6 %copy.11 = f32[192]{0:T(256)} copy(f32[192]{0:T(256)S(1)} %bitcast.7) | data formatting | bytes 1536
Async XLA Ops:
  45.9 0.7 %copy-start.1 = (f32[1,192]{1,0:T(1,128)S(1)}, f32[1,192]{1,0:T(1,128)}, u32[]{:S(2)}) copy-start(f32[1,192]{1,0:T(1,128)} %get-tuple-element.6) | copy-start | bytes 2308
  46.5 0.6 %copy-start = (f32[1,192]{1,0:T(1,128)S(1)}, f32[1,192]{1,0:T(1,128)}, u32[]{:S(2)}) copy-start(f32[1,192]{1,0:T(1,128)} %get-tuple-element.7) | copy-start | bytes 2308

commit v2 on v1

v2 whole, which is shorter than its diff:
```python
import functools
import math

import jax
import jax.numpy as jnp
from jax import lax
from jax.experimental import pallas as pl
from jax.experimental.pallas import tpu as pltpu
from jax.sharding import PartitionSpec as P

very_low = -1e30
floor = -1e29
IMAGE_PIECES = 4
CAPTION_PIECES = 4
LAST_PIECES = 2
HELD_BACK = 1
LANES = 128
SUBLANES = 8
log2_e = math.log2(math.e)
ln_2 = math.log(2)


def grid_of(blk, rep):
    chips = (blk // 2) * rep
    planes = 1
    while (planes * 2) ** 2 <= chips and (blk // 2) % (planes * 2) == 0:
        planes *= 2
    return planes, blk // 2 // planes


def mod(a, b):
    return a & (b - 1) if b & (b - 1) == 0 else lax.rem(a, b)


def div(a, b):
    return a >> (b.bit_length() - 1) if b & (b - 1) == 0 else lax.div(a, b)


def semaphore_counts(U, V, rep):
    H = U // 2
    along = (H - 1) * IMAGE_PIECES
    across = H * (V - 1) * IMAGE_PIECES
    return along, across, along + across + H, 2 * CAPTION_PIECES + (rep - 1) * (1 + LAST_PIECES)


def kernel(
    blk, rep, cap_ref, img_ref, pos_ref, val_ref, closs_ref, iloss_ref, loss_ref,
    mine, caps, imgs, raw, words, image_bias, image_ids, target, caption_bias,
    row_peak, row_total, row_match, col_peak, col_total, col_match,
    rowsend, rowrecv, colsend, colrecv, part, closs, iloss,
    loc_sem, out_sem, img_recv, cap_recv, send_sem, recv_sem,
):
    U, V = grid_of(blk, rep)
    N = blk * rep
    G = N // U
    H = U // 2
    B = V * 2
    n, width = cap_ref.shape
    C = B * n
    along_sems, across_sems, _, _ = semaphore_counts(U, V, rep)
    b, r = lax.axis_index("blk"), lax.axis_index("rep")
    c = mod(b, 2)
    u = div(b, 2 * V)
    v = mod(div(b, 2), V)
    me = b * rep + r
    g = mod(me, G)
    half, h = div(u, H), mod(u, H)
    keeps_own = div(u, 2) == h
    img_sent, cap_sent, line_sent, plane_sent, row_sent, col_sent, part_sent = (
        send_sem.at[k] for k in range(7)
    )
    line_came, plane_came, row_came, col_came, part_came = (recv_sem.at[k] for k in range(5))

    def near_of(uu):
        return jnp.where(uu > 2 * mod(uu, H), 1, 0)

    near = near_of(u)

    def member(uu, vv, cc, rr):
        return ((uu * V + vv) * 2 + cc) * rep + rr

    def remote(src, dst, ss, rs, to):
        return pltpu.make_async_remote_copy(
            src_ref=src, dst_ref=dst, send_sem=ss, recv_sem=rs, device_id=to,
            device_id_type=pl.DeviceIdType.LOGICAL,
        )

    partner = member(u, v, 1 - c, r)

    def sent(ref, sem):
        remote(ref, ref, sem, img_recv.at[0], partner).wait_send()

    def came(ref, sem):
        remote(ref, ref, img_sent, sem, partner).wait_recv()

    barrier = pltpu.get_barrier_semaphore()
    others = [u * G + mod(g + k, G) for k in range(1, G)]
    others += [mod(u + k, U) * G + g for k in range(1, U)]
    for to in others:
        pl.semaphore_signal(
            barrier, inc=1, device_id=to, device_id_type=pl.DeviceIdType.LOGICAL
        )

    def block(i, vv, cc):
        return (i * V + vv) * 2 + cc

    load_val = pltpu.make_async_copy(val_ref, raw.at[0], loc_sem.at[0])
    load_pos = pltpu.make_async_copy(pos_ref, raw.at[1], loc_sem.at[1])
    load_img = pltpu.make_async_copy(img_ref, imgs.at[block(h, v, c)], loc_sem.at[2])
    load_cap = pltpu.make_async_copy(cap_ref, mine, loc_sem.at[3])
    keep_cap = pltpu.make_async_copy(cap_ref, caps.at[0], loc_sem.at[4])
    load_val.start()
    load_pos.start()
    load_img.start()
    load_cap.start()

    @pl.when(keeps_own)
    def _():
        keep_cap.start()

    load_val.wait()
    load_pos.wait()
    words[g * U + u] = raw[1] * 2 + raw[0]
    load_img.wait()
    load_cap.wait()

    @pl.when(keeps_own)
    def _():
        keep_cap.wait()

    pl.semaphore_wait(barrier, len(others))

    def image_rows(k):
        return pl.ds(k * (n // IMAGE_PIECES), n // IMAGE_PIECES)

    def caption_rows(k):
        return pl.ds(k * (n // CAPTION_PIECES), n // CAPTION_PIECES)

    def img_copy(at, k, sem, to):
        rows = imgs.at[at, image_rows(k)]
        return remote(rows, rows, img_sent, img_recv.at[sem], to)

    def img_along(d, k):
        to = member(half * H + mod(h + d, H), v, c, r)
        return img_copy(block(h, v, c), k, (H - d - 1) * IMAGE_PIECES + k, to)

    def img_across(di, d, k):
        at = block(mod(h + di, H), v, c)
        sem = along_sems + (di * (V - 1) + V - d - 1) * IMAGE_PIECES + k
        return img_copy(at, k, sem, member(u, mod(v + d, V), c, r))

    def img_beside(di, vv, k):
        return img_copy(block(mod(h + di, H), vv, c), k, along_sems + across_sems + di, partner)

    def along_came(di, k):
        at = block(mod(h + di, H), v, c)
        came(imgs.at[at, image_rows(k)], img_recv.at[(di - 1) * IMAGE_PIECES + k])

    def across_came(di, d, k):
        at = block(mod(h + di, H), mod(v + d, V), c)
        sem = along_sems + (di * (V - 1) + d - 1) * IMAGE_PIECES + k
        came(imgs.at[at, image_rows(k)], img_recv.at[sem])

    def beside_came(di):
        came(imgs.at[pl.ds(mod(h + di, H) * B, V)], img_recv.at[along_sems + across_sems + di])

    def cap_along(t, k):
        rows = caption_rows(k)
        to = t * H + div(u, 2)
        away = jnp.where(mod(u, 2) == near_of(to), 0, 1)
        return remote(
            mine.at[rows], caps.at[away * rep, rows], cap_sent,
            cap_recv.at[away * CAPTION_PIECES + k], member(to, v, c, r),
        )

    def cap_across(away, d, k):
        rows = caption_rows(k)
        seat = rep - d
        sem = 2 * CAPTION_PIECES + seat - 1
        if away:
            piece = k // (CAPTION_PIECES // LAST_PIECES)
            sem = 2 * CAPTION_PIECES + rep - 1 + (seat - 1) * LAST_PIECES + piece
        return remote(
            caps.at[away * rep, rows], caps.at[away * rep + seat, rows], cap_sent,
            cap_recv.at[sem], member(u, v, c, mod(r + d, rep)),
        )

    def relay_captions(away, k):
        came(caps.at[away * rep, caption_rows(k)], cap_recv.at[away * CAPTION_PIECES + k])
        for d in range(1, rep):
            cap_across(away, d, k).start()

    def line_copy(k):
        row = words.at[g * U + u]
        return remote(row, row, line_sent, line_came, mod(u + k, U) * G + g)

    def plane_copy(k):
        rows = words.at[pl.ds(g * U, U)]
        return remote(rows, rows, plane_sent, plane_came, u * G + mod(g + k, G))

    def own_across(k):
        for d in range(1, V):
            img_across(0, d, k).start()

    def own_captions_across(k):
        @pl.when(keeps_own)
        def _():
            for d in range(1, rep):
                cap_across(0, d, k).start()

    for k in range(1, U):
        line_copy(k).start()
    for k in range(IMAGE_PIECES):
        for d in range(1, H):
            img_along(d, k).start()
        if k < IMAGE_PIECES - HELD_BACK:
            own_across(k)
        img_beside(0, v, k).start()
    for k in range(CAPTION_PIECES):
        for t in range(2):
            @pl.when(t * H + div(u, 2) != u)
            def _():
                cap_along(t, k).start()
        if k < CAPTION_PIECES - HELD_BACK:
            own_captions_across(k)

    for i in range(H):
        base = (half * H + i) * G
        for s in range(B):
            cols = slice(s * n, (s + 1) * n)
            first = (base + s * rep + r) * n
            image_ids[i, :, cols] = first + lax.broadcasted_iota(jnp.int32, (1, n), 1)
    col_peak[...] = jnp.full(col_peak.shape, floor, jnp.float32)
    col_total[...] = jnp.zeros(col_total.shape, jnp.float32)
    col_match[...] = jnp.zeros(col_match.shape, jnp.float32)
    row_peak[...] = jnp.full(row_peak.shape, floor, jnp.float32)
    row_total[...] = jnp.zeros(row_total.shape, jnp.float32)
    row_match[...] = jnp.zeros(row_match.shape, jnp.float32)

    came(words.at[pl.ds(0, U - 1)], line_came)
    for k in range(1, G):
        plane_copy(k).start()
    for k in range(IMAGE_PIECES - HELD_BACK, IMAGE_PIECES):
        own_across(k)
    for k in range(CAPTION_PIECES - HELD_BACK, CAPTION_PIECES):
        own_captions_across(k)

    for k in range(max(IMAGE_PIECES, CAPTION_PIECES)):
        if k < IMAGE_PIECES:
            for di in range(1, H):
                along_came(di, k)
                for d in range(1, V):
                    img_across(di, d, k).start()
                img_beside(di, v, k).start()
            for d in range(1, V):
                across_came(0, d, k)
                img_beside(0, mod(v + d, V), k).start()
        if k < CAPTION_PIECES:
            @pl.when(jnp.logical_not(keeps_own))
            def _():
                relay_captions(0, k)

    came(words.at[pl.ds(0, (G - 1) * U)], plane_came)

    eye = lax.broadcasted_iota(jnp.int32, (n, n), 0) == lax.broadcasted_iota(jnp.int32, (n, n), 1)

    def to_column(row):
        return jnp.sum(jnp.where(eye, row, 0.0), axis=1, keepdims=True)

    def to_row(column):
        return jnp.sum(jnp.where(eye, column, 0.0), axis=0, keepdims=True)

    flags = (words[:, 0, :] & 1).astype(jnp.float32)
    image_total = jnp.sum(jnp.sum(flags, axis=1, keepdims=True), axis=0, keepdims=True)

    def seat_row(s):
        away, d = div(s, rep), mod(s, rep)
        uu = 2 * h + jnp.where(away == 0, near, 1 - near)
        return ((v * 2 + c) * rep + mod(r + d, rep)) * U + uu

    aims = [words[seat_row(s)] >> 1 for s in range(2 * rep)] + [words[g * U + u] >> 1]
    aim = jnp.concatenate(aims, axis=1)
    order = lax.broadcasted_iota(jnp.int32, (N, aim.shape[1]), 0)
    starts = (mod(order, U) * G + div(order, U)) * n
    inside = (aim >= starts) & (aim < starts + n)
    picked = jnp.dot(
        flags.T.astype(jnp.bfloat16), jnp.where(inside, 1.0, 0.0).astype(jnp.bfloat16),
        preferred_element_type=jnp.float32,
    )
    start = jnp.sum(jnp.where(inside, starts, 0).astype(jnp.float32), axis=0, keepdims=True)
    low = aim - start.astype(jnp.int32)
    depth = lax.broadcasted_iota(jnp.int32, picked.shape, 0)
    ok = jnp.sum(jnp.where(depth == low, picked, 0.0), axis=0, keepdims=True)
    own_ok = ok[:, 2 * rep * n :]
    for s in range(2 * rep):
        ok_row = ok[:, s * n : (s + 1) * n]
        bias = to_column(jnp.where(ok_row > 0, 0.0, very_low))
        caption_bias[s] = jnp.broadcast_to(bias, (n, LANES))
        aim_column = to_column(aims[s].astype(jnp.float32)).astype(jnp.int32)
        target[s] = jnp.broadcast_to(aim_column, (n, LANES))
    for i in range(H):
        for s in range(B):
            flag = words[(s * rep + r) * U + half * H + i] & 1
            image_bias[i, :, s * n : (s + 1) * n] = jnp.where(flag > 0, 0.0, very_low)

    def fold(x, op):
        y = x[:, :LANES]
        for j in range(1, C // LANES):
            y = op(y, x[:, j * LANES : (j + 1) * LANES])
        return y

    def wide(x):
        return jnp.concatenate([x] * (C // LANES), axis=1)

    def tally(s, i, scores, first, rows):
        scaled = scores * log2_e
        bias, ids = image_bias[i], image_ids[i]
        old_peak = col_peak[i]
        peak, match = old_peak, col_match[i]
        peaks = []
        for q in range(rows // SUBLANES):
            at = pl.ds(first + q * SUBLANES, SUBLANES)
            x = scaled[q * SUBLANES : (q + 1) * SUBLANES]
            peaks.append(jnp.maximum(fold(x + bias, jnp.maximum), row_peak[s, at]))
            peak = jnp.maximum(peak, x + wide(caption_bias[s, at]))
            picked = jnp.where(wide(target[s, at]) == ids, x, 0.0)
            row_match[s, at] = row_match[s, at] + fold(picked, jnp.add)
            match = match + picked
        total = col_total[i] * jnp.exp2(old_peak - peak)
        for q in range(rows // SUBLANES):
            at = pl.ds(first + q * SUBLANES, SUBLANES)
            x = scaled[q * SUBLANES : (q + 1) * SUBLANES]
            powers = jnp.exp2(x + bias - wide(peaks[q]))
            row_total[s, at] = row_total[s, at] * jnp.exp2(row_peak[s, at] - peaks[q]) + fold(
                powers, jnp.add
            )
            row_peak[s, at] = peaks[q]
            total = total + jnp.exp2(x + wide(caption_bias[s, at]) - peak)
        col_peak[i] = peak
        col_total[i] = total
        col_match[i] = match

    def score(s, count, i, first, rows):
        left = caps[pl.ds(s, count)].reshape(count * n, width) if rows == n else caps[s, pl.ds(first, rows)]
        scores = lax.dot_general(
            left, imgs[pl.ds(i * B, B)].reshape(C, width), (((1,), (1,)), ((), ())),
            preferred_element_type=jnp.float32,
        )
        for k in range(count):
            tally(s + k, i, scores[k * rows : (k + 1) * rows], first, rows)

    beside_came(0)

    @pl.loop(0, rep + 1)
    def _(e):
        for k in range(max(CAPTION_PIECES, IMAGE_PIECES)):
            @pl.when(e == min(k, rep))
            def _():
                if k < CAPTION_PIECES:
                    relay_captions(1, k)
                if k < IMAGE_PIECES:
                    for di in range(1, H):
                        for d in range(1, V):
                            across_came(di, d, k)
                            img_beside(di, mod(v + d, V), k).start()

        @pl.when((e > 0) & (e < rep))
        def _():
            came(caps.at[0], cap_recv.at[2 * CAPTION_PIECES + e - 1])
        score(e, 1, h, 0, n)

    @pl.loop(1, H)
    def _(di):
        beside_came(di)
        score(0, rep + 1, mod(h + di, H), 0, n)

    def row_copy(s):
        away, d = div(s, rep), mod(s, rep)
        uu = 2 * h + jnp.where(away == 0, near, 1 - near)
        at = half * rep + r
        return remote(
            rowsend.at[s], rowrecv.at[at], row_sent, row_came, member(uu, v, c, mod(r + d, rep))
        )

    def send_rows(s):
        peak = jnp.max(row_peak[s], axis=1, keepdims=True)
        total = jnp.sum(row_total[s] * jnp.exp2(row_peak[s] - peak), axis=1, keepdims=True)
        rowsend[s, 0:1, :] = to_row(peak)
        rowsend[s, 1:2, :] = to_row(total)
        rowsend[s, 2:3, :] = to_row(jnp.sum(row_match[s], axis=1, keepdims=True))
        stays = keeps_own & (s == 0)

        @pl.when(jnp.logical_not(stays))
        def _():
            row_copy(s).start()

        @pl.when(stays)
        def _():
            rowrecv[half * rep + r] = rowsend[s]

    @pl.loop(0, rep + 1)
    def _(s):
        send_rows(s)

    @pl.loop(1, rep)
    def _(d):
        @pl.loop(0, LAST_PIECES)
        def _(k):
            rows = n // LAST_PIECES
            came(
                caps.at[rep + d, pl.ds(0, rows)],
                cap_recv.at[2 * CAPTION_PIECES + rep - 1 + (d - 1) * LAST_PIECES + k],
            )

            @pl.loop(0, H)
            def _(e):
                score(rep + d, 1, e, k * rows, rows)
        send_rows(rep + d)

    own_at = h * B + v * 2 + c
    for i in range(H):
        peak = jnp.max(col_peak[i], axis=0, keepdims=True)
        total = jnp.sum(col_total[i] * jnp.exp2(col_peak[i] - peak), axis=0, keepdims=True)
        match = jnp.sum(col_match[i], axis=0, keepdims=True)
        for s in range(B):
            cols = slice(s * n, (s + 1) * n)
            colsend[i * B + s, 0:1, :] = peak[:, cols]
            colsend[i * B + s, 1:2, :] = total[:, cols]
            colsend[i * B + s, 2:3, :] = match[:, cols]

    def col_copy(k):
        slot = mod(own_at + k, H * B)
        i, s = div(slot, B), mod(slot, B)
        to = (half * H + i) * G + s * rep + r
        return remote(colsend.at[slot], colrecv.at[own_at], col_sent, col_came, to)

    for k in range(1, H * B):
        col_copy(k).start()
    colrecv[own_at] = colsend[own_at]

    def joined(parts, count):
        peak = parts[0, 0:1, :]
        for s in range(1, count):
            peak = jnp.maximum(peak, parts[s, 0:1, :])
        total = jnp.zeros_like(peak)
        match = jnp.zeros_like(peak)
        for s in range(count):
            total += parts[s, 1:2, :] * jnp.exp2(parts[s, 0:1, :] - peak)
            match += parts[s, 2:3, :]
        return (peak - match) * ln_2 + jnp.log(total)

    @pl.when(keeps_own)
    def _():
        came(rowrecv.at[pl.ds(0, 2 * rep - 1)], row_came)

    @pl.when(jnp.logical_not(keeps_own))
    def _():
        came(rowrecv, row_came)

    caption_loss = own_ok * joined(rowrecv, 2 * rep)
    closs[...] = caption_loss
    put_caption = pltpu.make_async_copy(closs, closs_ref, out_sem.at[0])
    put_caption.start()
    came(colrecv.at[pl.ds(0, H * B - 1)], col_came)
    image_loss = raw[0].astype(jnp.float32) * joined(colrecv, H * B)
    iloss[...] = image_loss
    put_image = pltpu.make_async_copy(iloss, iloss_ref, out_sem.at[1])
    put_image.start()
    own_sum = jnp.sum(caption_loss + image_loss, axis=1, keepdims=True)
    part[me] = jnp.broadcast_to(own_sum, (1, LANES))

    @pl.loop(1, N)
    def _(k):
        remote(part.at[me], part.at[me], part_sent, part_came, mod(me + k, N)).start()

    sent(words.at[pl.ds(0, U - 1)], line_sent)
    sent(words.at[pl.ds(0, (G - 1) * U)], plane_sent)
    sent(imgs.at[pl.ds(0, H * B - 1)], img_sent)

    @pl.when(keeps_own)
    def _():
        sent(caps.at[pl.ds(0, 2 * rep - 1)], cap_sent)
        sent(rowsend.at[pl.ds(0, 2 * rep - 1)], row_sent)

    @pl.when(jnp.logical_not(keeps_own))
    def _():
        sent(caps, cap_sent)
        sent(rowsend, row_sent)

    sent(colsend.at[pl.ds(0, H * B - 1)], col_sent)
    put_caption.wait()
    put_image.wait()
    sent(part.at[pl.ds(0, N - 1)], part_sent)
    came(part.at[pl.ds(0, N - 1)], part_came)

    whole = jnp.sum(part[:, 0, :], axis=0, keepdims=True)
    loss_ref[...] = whole[:, 0:1] / (2.0 * image_total)


def local(blk, rep, captions, images, positives, valid):
    n, width = captions.shape
    U, V = grid_of(blk, rep)
    N = blk * rep
    H, B = U // 2, V * 2
    C = B * n
    f32, i32 = jnp.float32, jnp.int32
    _, _, image_sems, caption_sems = semaphore_counts(U, V, rep)
    dma = lambda count: pltpu.SemaphoreType.DMA((count,))
    vmem = pl.BlockSpec(memory_space=pltpu.VMEM)
    hbm = pl.BlockSpec(memory_space=pl.ANY)
    caption_loss, image_loss, loss = pl.pallas_call(
        functools.partial(kernel, blk, rep),
        out_shape=(
            jax.ShapeDtypeStruct((1, n), f32),
            jax.ShapeDtypeStruct((1, n), f32),
            jax.ShapeDtypeStruct((1, 1), f32),
        ),
        in_specs=[hbm] * 4,
        out_specs=(hbm, hbm, vmem),
        scratch_shapes=[
            pltpu.VMEM((n, width), captions.dtype),
            pltpu.VMEM((2 * rep, n, width), captions.dtype),
            pltpu.VMEM((H * B, n, width), images.dtype),
            pltpu.VMEM((2, 1, n), i32),
            pltpu.VMEM((N, 1, n), i32),
            pltpu.VMEM((H, 1, C), f32),
            pltpu.VMEM((H, 1, C), i32),
            pltpu.VMEM((2 * rep, n, LANES), i32),
            pltpu.VMEM((2 * rep, n, LANES), f32),
            pltpu.VMEM((2 * rep, n, LANES), f32),
            pltpu.VMEM((2 * rep, n, LANES), f32),
            pltpu.VMEM((2 * rep, n, LANES), f32),
            pltpu.VMEM((H, SUBLANES, C), f32),
            pltpu.VMEM((H, SUBLANES, C), f32),
            pltpu.VMEM((H, SUBLANES, C), f32),
            pltpu.VMEM((2 * rep, 8, n), f32),
            pltpu.VMEM((2 * rep, 8, n), f32),
            pltpu.VMEM((H * B, 8, n), f32),
            pltpu.VMEM((H * B, 8, n), f32),
            pltpu.VMEM((N, 1, LANES), f32),
            pltpu.VMEM((1, n), f32),
            pltpu.VMEM((1, n), f32),
            dma(5), dma(2), dma(image_sems), dma(caption_sems), dma(7), dma(5),
        ],
        compiler_params=pltpu.CompilerParams(collective_id=0, has_side_effects=True),
    )(captions, images, positives.reshape(1, n), valid.reshape(1, n))
    return caption_loss.reshape(n), image_loss.reshape(n), loss.reshape(())


def solution(mesh):
    placed = (
        P(("blk", "rep"), None),
        P(("blk", "rep"), None),
        P(("blk", "rep")),
        P(("blk", "rep")),
    )
    return jax.shard_map(
        functools.partial(local, mesh.shape["blk"], mesh.shape["rep"]),
        mesh=mesh,
        in_specs=placed,
        out_specs=(P(("blk", "rep")), P(("blk", "rep")), P()),
        check_vma=False,
    )
```

time: 49.7 us -> 39.6 us (0.80)
  Pallas kernels: 45.2 us -> 35.1 us
    pallas_call x1, Pallas kernels: 45.2 us -> 35.1 us  [local(): pl.pallas_call(functools.partial(kernel, blk, rep), out_shape=(jax.ShapeD...]
where the time goes in v2:
time: 39.6 us; the launch traced here: 39.4 us
  Pallas kernels  35.1 us (89%)
  between operations  2.4 us (6%)
  local copies, waits for them, and re-layouts  1.86 us (5%)
    pallas_call x1, Pallas kernels, local(): pl.pallas_call(functools.partial(kernel, blk, rep), out_shape=(jax.ShapeD...  35.1 us
    unnamed x6, local copies, waits for them, and re-layouts  1.86 us

profile of v2, /device:TPU:0, one launch (start us, length us, event | category | flops | bytes accessed | tf_op | source)
XLA Modules:
  0.0 39.4 jit_solution(4268202314227598919)
XLA Ops:
  0.6 35.1 %shard_map.67 = (f32[1,192]{1,0:T(1,128)}, f32[1,192]{1,0:T(1,128)}, f32[1,1]{1,0:T(1,128)}) custom-call(bf16[192,768]{1,0:T(8,128)(2,1)} %cap_ref.1, bf16[192,768]{1,0:T(8,128)(2,1)} %img_ref.1, s32[1,192]{1,0:T(1,128)} %bitcast.5, s32[1,192]{1,0:T(1,128)} %bitcast.6), custom_call_target="tpu_custom_call" | custom-call | tf_op jit(solution)/shard_map/pallas_call | solution.py:511
  35.8 0.0 copy-start.1
  35.8 0.7 %copy-done.1 = f32[1,192]{1,0:T(1,128)S(1)} copy-done((f32[1,192]{1,0:T(1,128)S(1)}, f32[1,192]{1,0:T(1,128)}, u32[]{:S(2)}) %copy-start.1) | copy-done | bytes 792
  36.4 0.0 copy-start
  36.4 0.6 %copy.10 = f32[192]{0:T(256)} copy(f32[192]{0:T(256)S(1)} %bitcast.8) | data formatting | bytes 1536
  37.0 0.1 copy-done
  37.1 0.6 %copy.11 = f32[192]{0:T(256)} copy(f32[192]{0:T(256)S(1)} %bitcast.7) | data formatting | bytes 1536
Async XLA Ops:
  35.8 0.7 %copy-start.1 = (f32[1,192]{1,0:T(1,128)S(1)}, f32[1,192]{1,0:T(1,128)}, u32[]{:S(2)}) copy-start(f32[1,192]{1,0:T(1,128)} %get-tuple-element.6) | copy-start | bytes 2308
  36.4 0.6 %copy-start = (f32[1,192]{1,0:T(1,128)S(1)}, f32[1,192]{1,0:T(1,128)}, u32[]{:S(2)}) copy-start(f32[1,192]{1,0:T(1,128)} %get-tuple-element.7) | copy-start | bytes 2308

commit v3 on v2

--- a/solution.py
+++ b/solution.py
@@ -44,11 +44,11 @@
 
 
 def kernel(
-    blk, rep, cap_ref, img_ref, pos_ref, val_ref, closs_ref, iloss_ref, loss_ref,
+    blk, rep, cap_ref, img_ref, pos_ref, val_ref, terms_ref,
     mine, caps, imgs, raw, words, image_bias, image_ids, target, caption_bias,
     row_peak, row_total, row_match, col_peak, col_total, col_match,
-    rowsend, rowrecv, colsend, colrecv, part, closs, iloss,
-    loc_sem, out_sem, img_recv, cap_recv, send_sem, recv_sem,
+    rowsend, rowrecv, colsend, colrecv, part,
+    loc_sem, img_recv, cap_recv, send_sem, recv_sem,
 ):
     U, V = grid_of(blk, rep)
     N = blk * rep
@@ -458,14 +458,10 @@
         came(rowrecv, row_came)
 
     caption_loss = own_ok * joined(rowrecv, 2 * rep)
-    closs[...] = caption_loss
-    put_caption = pltpu.make_async_copy(closs, closs_ref, out_sem.at[0])
-    put_caption.start()
+    terms_ref[0:1, :] = caption_loss
     came(colrecv.at[pl.ds(0, H * B - 1)], col_came)
     image_loss = raw[0].astype(jnp.float32) * joined(colrecv, H * B)
-    iloss[...] = image_loss
-    put_image = pltpu.make_async_copy(iloss, iloss_ref, out_sem.at[1])
-    put_image.start()
+    terms_ref[1:2, :] = image_loss
     own_sum = jnp.sum(caption_loss + image_loss, axis=1, keepdims=True)
     part[me] = jnp.broadcast_to(own_sum, (1, LANES))
 
@@ -488,13 +484,17 @@
         sent(rowsend, row_sent)
 
     sent(colsend.at[pl.ds(0, H * B - 1)], col_sent)
-    put_caption.wait()
-    put_image.wait()
     sent(part.at[pl.ds(0, N - 1)], part_sent)
     came(part.at[pl.ds(0, N - 1)], part_came)
 
     whole = jnp.sum(part[:, 0, :], axis=0, keepdims=True)
-    loss_ref[...] = whole[:, 0:1] / (2.0 * image_total)
+    terms_ref[2:3, 0:1] = whole[:, 0:1] / (2.0 * image_total)
+
+
+def hand_out(terms_ref, closs_ref, iloss_ref, loss_ref):
+    closs_ref[...] = terms_ref[0:1, :]
+    iloss_ref[...] = terms_ref[1:2, :]
+    loss_ref[...] = terms_ref[2:3, 0:1]
 
 
 def local(blk, rep, captions, images, positives, valid):
@@ -508,15 +508,11 @@
     dma = lambda count: pltpu.SemaphoreType.DMA((count,))
     vmem = pl.BlockSpec(memory_space=pltpu.VMEM)
     hbm = pl.BlockSpec(memory_space=pl.ANY)
-    caption_loss, image_loss, loss = pl.pallas_call(
+    terms = pl.pallas_call(
         functools.partial(kernel, blk, rep),
-        out_shape=(
-            jax.ShapeDtypeStruct((1, n), f32),
-            jax.ShapeDtypeStruct((1, n), f32),
-            jax.ShapeDtypeStruct((1, 1), f32),
-        ),
+        out_shape=pltpu.VMEM((SUBLANES, n), f32),
         in_specs=[hbm] * 4,
-        out_specs=(hbm, hbm, vmem),
+        out_specs=vmem,
         scratch_shapes=[
             pltpu.VMEM((n, width), captions.dtype),
             pltpu.VMEM((2 * rep, n, width), captions.dtype),
@@ -538,12 +534,20 @@
             pltpu.VMEM((H * B, 8, n), f32),
             pltpu.VMEM((H * B, 8, n), f32),
             pltpu.VMEM((N, 1, LANES), f32),
-            pltpu.VMEM((1, n), f32),
-            pltpu.VMEM((1, n), f32),
-            dma(5), dma(2), dma(image_sems), dma(caption_sems), dma(7), dma(5),
+            dma(5), dma(image_sems), dma(caption_sems), dma(7), dma(5),
         ],
         compiler_params=pltpu.CompilerParams(collective_id=0, has_side_effects=True),
     )(captions, images, positives.reshape(1, n), valid.reshape(1, n))
+    caption_loss, image_loss, loss = pl.pallas_call(
+        hand_out,
+        out_shape=(
+            jax.ShapeDtypeStruct((1, n), f32),
+            jax.ShapeDtypeStruct((1, n), f32),
+            jax.ShapeDtypeStruct((1, 1), f32),
+        ),
+        in_specs=[vmem],
+        out_specs=(vmem,) * 3,
+    )(pltpu.with_memory_space_constraint(terms, pltpu.VMEM))
     return caption_loss.reshape(n), image_loss.reshape(n), loss.reshape(())
 
 

time: 39.6 us -> 35.9 us (0.907)
  local copies, waits for them, and re-layouts: 1.86 us -> 0 us
  between operations: 2.4 us -> 0.64 us
    unnamed x6 -> x0, local copies, waits for them, and re-layouts: 1.86 us -> none
    pallas_call x1 -> x2, Pallas kernels: 35.1 us -> 35.1 us  [the longest x1 34.6 us: local(): pl.pallas_call(functools.partial(kernel, blk, rep), out_shape=pltpu.VMEM(...]
where the time goes in v3:
time: 35.9 us; the launch traced here: 35.8 us
  Pallas kernels  35.1 us (98%)
  between operations  0.64 us (2%)
    pallas_call x1, Pallas kernels, local(): pl.pallas_call(functools.partial(kernel, blk, rep), out_shape=pltpu.VMEM(...  34.6 us

profile of v3, /device:TPU:0, one launch (start us, length us, event | category | flops | bytes accessed | tf_op | source)
XLA Modules:
  0.0 35.8 jit_solution(3966572346221926744)
XLA Ops:
  0.6 34.6 %shard_map.67.terms_ref = f32[8,192]{1,0:T(8,128)S(1)} custom-call(bf16[192,768]{1,0:T(8,128)(2,1)} %cap_ref.1, bf16[192,768]{1,0:T(8,128)(2,1)} %img_ref.1, s32[1,192]{1,0:T(1,128)} %bitcast.5, s32[1,192]{1,0:T(1,128)} %bitcast.6), custom_call_target="tpu_custom_call" | custom-call | tf_op jit(solution)/shard_map/pallas_call | solution.py:511
  35.2 0.6 %shard_map.68 = (f32[1,192]{1,0:T(1,128)}, f32[1,192]{1,0:T(1,128)}, f32[1,1]{1,0:T(1,128)}) custom-call(f32[8,192]{1,0:T(8,128)S(1)} %shard_map.67.terms_ref), custom_call_target="tpu_custom_call" | custom-call | tf_op jit(solution)/shard_map/pallas_call | solution.py:541

commit v4 on v3

--- a/solution.py
+++ b/solution.py
@@ -11,9 +11,10 @@
 very_low = -1e30
 floor = -1e29
 IMAGE_PIECES = 4
-CAPTION_PIECES = 4
+CAPTION_PIECES = 6
 LAST_PIECES = 2
-HELD_BACK = 1
+IMAGES_HELD = 1
+CAPTIONS_HELD = 2
 LANES = 128
 SUBLANES = 8
 log2_e = math.log2(math.e)
@@ -40,7 +41,15 @@
     H = U // 2
     along = (H - 1) * IMAGE_PIECES
     across = H * (V - 1) * IMAGE_PIECES
-    return along, across, along + across + H, 2 * CAPTION_PIECES + (rep - 1) * (1 + LAST_PIECES)
+    return along, across, along + across + H * V, 2 * CAPTION_PIECES + (rep - 1) * (1 + LAST_PIECES)
+
+
+def group_at(V, H, di, dv):
+    if di == 0:
+        return dv
+    if dv == 0:
+        return V + di - 1
+    return V + H - 1 + (di - 1) * (V - 1) + dv - 1
 
 
 def kernel(
@@ -56,7 +65,8 @@
     H = U // 2
     B = V * 2
     n, width = cap_ref.shape
-    C = B * n
+    early = (V + H - 1) * 2 * n
+    C = H * B * n
     along_sems, across_sems, _, _ = semaphore_counts(U, V, rep)
     b, r = lax.axis_index("blk"), lax.axis_index("rep")
     c = mod(b, 2)
@@ -101,12 +111,17 @@
             barrier, inc=1, device_id=to, device_id_type=pl.DeviceIdType.LOGICAL
         )
 
-    def block(i, vv, cc):
-        return (i * V + vv) * 2 + cc
+    def group(di, dv):
+        return group_at(V, H, di, dv)
+
+    offsets = sorted((group(di, dv), di, dv) for di in range(H) for dv in range(V))
+
+    def image_member(di, dv, k):
+        return member(half * H + mod(h + di, H), mod(v + dv, V), c if k == 0 else 1 - c, r)
 
     load_val = pltpu.make_async_copy(val_ref, raw.at[0], loc_sem.at[0])
     load_pos = pltpu.make_async_copy(pos_ref, raw.at[1], loc_sem.at[1])
-    load_img = pltpu.make_async_copy(img_ref, imgs.at[block(h, v, c)], loc_sem.at[2])
+    load_img = pltpu.make_async_copy(img_ref, imgs.at[0], loc_sem.at[2])
     load_cap = pltpu.make_async_copy(cap_ref, mine, loc_sem.at[3])
     keep_cap = pltpu.make_async_copy(cap_ref, caps.at[0], loc_sem.at[4])
     load_val.start()
@@ -136,33 +151,35 @@
     def caption_rows(k):
         return pl.ds(k * (n // CAPTION_PIECES), n // CAPTION_PIECES)
 
-    def img_copy(at, k, sem, to):
-        rows = imgs.at[at, image_rows(k)]
-        return remote(rows, rows, img_sent, img_recv.at[sem], to)
+    def img_copy(at, to_at, k, sem, to):
+        rows = image_rows(k)
+        return remote(imgs.at[at, rows], imgs.at[to_at, rows], img_sent, img_recv.at[sem], to)
+
+    def across_sem(di, dv, k):
+        return along_sems + (di * (V - 1) + dv - 1) * IMAGE_PIECES + k
 
     def img_along(d, k):
         to = member(half * H + mod(h + d, H), v, c, r)
-        return img_copy(block(h, v, c), k, (H - d - 1) * IMAGE_PIECES + k, to)
+        return img_copy(0, group(H - d, 0) * 2, k, (H - d - 1) * IMAGE_PIECES + k, to)
 
     def img_across(di, d, k):
-        at = block(mod(h + di, H), v, c)
-        sem = along_sems + (di * (V - 1) + V - d - 1) * IMAGE_PIECES + k
-        return img_copy(at, k, sem, member(u, mod(v + d, V), c, r))
-
-    def img_beside(di, vv, k):
-        return img_copy(block(mod(h + di, H), vv, c), k, along_sems + across_sems + di, partner)
+        to = member(u, mod(v + d, V), c, r)
+        return img_copy(
+            group(di, 0) * 2, group(di, V - d) * 2, k, across_sem(di, V - d, k), to
+        )
+
+    def img_beside(di, dv, k):
+        at = group(di, dv)
+        return img_copy(at * 2, at * 2 + 1, k, along_sems + across_sems + at, partner)
 
     def along_came(di, k):
-        at = block(mod(h + di, H), v, c)
-        came(imgs.at[at, image_rows(k)], img_recv.at[(di - 1) * IMAGE_PIECES + k])
-
-    def across_came(di, d, k):
-        at = block(mod(h + di, H), mod(v + d, V), c)
-        sem = along_sems + (di * (V - 1) + d - 1) * IMAGE_PIECES + k
-        came(imgs.at[at, image_rows(k)], img_recv.at[sem])
-
-    def beside_came(di):
-        came(imgs.at[pl.ds(mod(h + di, H) * B, V)], img_recv.at[along_sems + across_sems + di])
+        came(imgs.at[group(di, 0) * 2, image_rows(k)], img_recv.at[(di - 1) * IMAGE_PIECES + k])
+
+    def across_came(di, dv, k):
+        came(imgs.at[group(di, dv) * 2, image_rows(k)], img_recv.at[across_sem(di, dv, k)])
+
+    def beside_came(at):
+        came(imgs.at[at * 2 + 1], img_recv.at[along_sems + across_sems + at])
 
     def cap_along(t, k):
         rows = caption_rows(k)
@@ -213,23 +230,22 @@
     for k in range(IMAGE_PIECES):
         for d in range(1, H):
             img_along(d, k).start()
-        if k < IMAGE_PIECES - HELD_BACK:
+        if k < IMAGE_PIECES - IMAGES_HELD:
             own_across(k)
-        img_beside(0, v, k).start()
+        img_beside(0, 0, k).start()
     for k in range(CAPTION_PIECES):
         for t in range(2):
             @pl.when(t * H + div(u, 2) != u)
             def _():
                 cap_along(t, k).start()
-        if k < CAPTION_PIECES - HELD_BACK:
+        if k < CAPTION_PIECES - CAPTIONS_HELD:
             own_captions_across(k)
 
-    for i in range(H):
-        base = (half * H + i) * G
-        for s in range(B):
-            cols = slice(s * n, (s + 1) * n)
-            first = (base + s * rep + r) * n
-            image_ids[i, :, cols] = first + lax.broadcasted_iota(jnp.int32, (1, n), 1)
+    for at, di, dv in offsets:
+        for k in range(2):
+            cols = slice((at * 2 + k) * n, (at * 2 + k + 1) * n)
+            first = image_member(di, dv, k) * n
+            image_ids[:, cols] = first + lax.broadcasted_iota(jnp.int32, (1, n), 1)
     col_peak[...] = jnp.full(col_peak.shape, floor, jnp.float32)
     col_total[...] = jnp.zeros(col_total.shape, jnp.float32)
     col_match[...] = jnp.zeros(col_match.shape, jnp.float32)
@@ -240,25 +256,28 @@
     came(words.at[pl.ds(0, U - 1)], line_came)
     for k in range(1, G):
         plane_copy(k).start()
-    for k in range(IMAGE_PIECES - HELD_BACK, IMAGE_PIECES):
+    for k in range(IMAGE_PIECES - IMAGES_HELD, IMAGE_PIECES):
         own_across(k)
-    for k in range(CAPTION_PIECES - HELD_BACK, CAPTION_PIECES):
+    for k in range(CAPTION_PIECES - CAPTIONS_HELD, CAPTION_PIECES):
         own_captions_across(k)
 
-    for k in range(max(IMAGE_PIECES, CAPTION_PIECES)):
-        if k < IMAGE_PIECES:
+    pieces = [((k + 1) / IMAGE_PIECES, 0, k) for k in range(IMAGE_PIECES)]
+    pieces += [((k + 1) / CAPTION_PIECES, 1, k) for k in range(CAPTION_PIECES)]
+    pieces.sort()
+    for _, is_caption, k in pieces:
+        if is_caption:
+            @pl.when(jnp.logical_not(keeps_own))
+            def _():
+                relay_captions(0, k)
+        else:
             for di in range(1, H):
                 along_came(di, k)
                 for d in range(1, V):
                     img_across(di, d, k).start()
-                img_beside(di, v, k).start()
-            for d in range(1, V):
-                across_came(0, d, k)
-                img_beside(0, mod(v + d, V), k).start()
-        if k < CAPTION_PIECES:
-            @pl.when(jnp.logical_not(keeps_own))
-            def _():
-                relay_captions(0, k)
+                img_beside(di, 0, k).start()
+            for dv in range(1, V):
+                across_came(0, dv, k)
+                img_beside(0, dv, k).start()
 
     came(words.at[pl.ds(0, (G - 1) * U)], plane_came)
 
@@ -298,25 +317,25 @@
         caption_bias[s] = jnp.broadcast_to(bias, (n, LANES))
         aim_column = to_column(aims[s].astype(jnp.float32)).astype(jnp.int32)
         target[s] = jnp.broadcast_to(aim_column, (n, LANES))
-    for i in range(H):
-        for s in range(B):
-            flag = words[(s * rep + r) * U + half * H + i] & 1
-            image_bias[i, :, s * n : (s + 1) * n] = jnp.where(flag > 0, 0.0, very_low)
+    for at, di, dv in offsets:
+        for k in range(2):
+            to = image_member(di, dv, k)
+            flag = words[mod(to, G) * U + div(to, G)] & 1
+            cols = slice((at * 2 + k) * n, (at * 2 + k + 1) * n)
+            image_bias[:, cols] = jnp.where(flag > 0, 0.0, very_low)
 
     def fold(x, op):
         y = x[:, :LANES]
-        for j in range(1, C // LANES):
+        for j in range(1, x.shape[1] // LANES):
             y = op(y, x[:, j * LANES : (j + 1) * LANES])
         return y
 
-    def wide(x):
-        return jnp.concatenate([x] * (C // LANES), axis=1)
-
-    def tally(s, i, scores, first, rows):
+    def tally(s, cols, scores, first, rows):
         scaled = scores * log2_e
-        bias, ids = image_bias[i], image_ids[i]
-        old_peak = col_peak[i]
-        peak, match = old_peak, col_match[i]
+        bias, ids = image_bias[:, cols], image_ids[:, cols]
+        old_peak = col_peak[:, cols]
+        peak, match = old_peak, col_match[:, cols]
+        wide = lambda x: jnp.concatenate([x] * (scores.shape[1] // LANES), axis=1)
         peaks = []
         for q in range(rows // SUBLANES):
             at = pl.ds(first + q * SUBLANES, SUBLANES)
@@ -326,7 +345,7 @@
             picked = jnp.where(wide(target[s, at]) == ids, x, 0.0)
             row_match[s, at] = row_match[s, at] + fold(picked, jnp.add)
             match = match + picked
-        total = col_total[i] * jnp.exp2(old_peak - peak)
+        total = col_total[:, cols] * jnp.exp2(old_peak - peak)
         for q in range(rows // SUBLANES):
             at = pl.ds(first + q * SUBLANES, SUBLANES)
             x = scaled[q * SUBLANES : (q + 1) * SUBLANES]
@@ -336,43 +355,47 @@
             )
             row_peak[s, at] = peaks[q]
             total = total + jnp.exp2(x + wide(caption_bias[s, at]) - peak)
-        col_peak[i] = peak
-        col_total[i] = total
-        col_match[i] = match
-
-    def score(s, count, i, first, rows):
-        left = caps[pl.ds(s, count)].reshape(count * n, width) if rows == n else caps[s, pl.ds(first, rows)]
+        col_peak[:, cols] = peak
+        col_total[:, cols] = total
+        col_match[:, cols] = match
+
+    def score(s, count, start, stop, first, rows):
+        left = caps[pl.ds(s, count), pl.ds(first, rows)].reshape(count * rows, width)
+        right = imgs[start // n : stop // n].reshape(stop - start, width)
         scores = lax.dot_general(
-            left, imgs[pl.ds(i * B, B)].reshape(C, width), (((1,), (1,)), ((), ())),
-            preferred_element_type=jnp.float32,
+            left, right, (((1,), (1,)), ((), ())), preferred_element_type=jnp.float32
         )
         for k in range(count):
-            tally(s + k, i, scores[k * rows : (k + 1) * rows], first, rows)
-
-    beside_came(0)
+            tally(s + k, slice(start, stop), scores[k * rows : (k + 1) * rows], first, rows)
+
+    for at in range(early // (2 * n)):
+        beside_came(at)
 
     @pl.loop(0, rep + 1)
     def _(e):
-        for k in range(max(CAPTION_PIECES, IMAGE_PIECES)):
-            @pl.when(e == min(k, rep))
+        for step in range(rep + 1):
+            @pl.when(e == step)
             def _():
-                if k < CAPTION_PIECES:
-                    relay_captions(1, k)
-                if k < IMAGE_PIECES:
-                    for di in range(1, H):
-                        for d in range(1, V):
-                            across_came(di, d, k)
-                            img_beside(di, mod(v + d, V), k).start()
+                for share, is_caption, k in pieces:
+                    if min(rep, 1 + math.ceil(share * rep - 1) if k else is_caption ^ 1) != step:
+                        continue
+                    if is_caption:
+                        relay_captions(1, k)
+                    else:
+                        for di in range(1, H):
+                            for dv in range(1, V):
+                                across_came(di, dv, k)
+                                img_beside(di, dv, k).start()
 
         @pl.when((e > 0) & (e < rep))
         def _():
             came(caps.at[0], cap_recv.at[2 * CAPTION_PIECES + e - 1])
-        score(e, 1, h, 0, n)
-
-    @pl.loop(1, H)
-    def _(di):
-        beside_came(di)
-        score(0, rep + 1, mod(h + di, H), 0, n)
+        score(e, 1, 0, early, 0, n)
+
+    for at in range(early // (2 * n), H * V):
+        beside_came(at)
+    if early < C:
+        score(0, rep + 1, early, C, 0, n)
 
     def row_copy(s):
         away, d = div(s, rep), mod(s, rep)
@@ -412,31 +435,26 @@
                 cap_recv.at[2 * CAPTION_PIECES + rep - 1 + (d - 1) * LAST_PIECES + k],
             )
 
-            @pl.loop(0, H)
-            def _(e):
-                score(rep + d, 1, e, k * rows, rows)
+            score(rep + d, 1, 0, C, k * rows, rows)
         send_rows(rep + d)
 
-    own_at = h * B + v * 2 + c
-    for i in range(H):
-        peak = jnp.max(col_peak[i], axis=0, keepdims=True)
-        total = jnp.sum(col_total[i] * jnp.exp2(col_peak[i] - peak), axis=0, keepdims=True)
-        match = jnp.sum(col_match[i], axis=0, keepdims=True)
-        for s in range(B):
-            cols = slice(s * n, (s + 1) * n)
-            colsend[i * B + s, 0:1, :] = peak[:, cols]
-            colsend[i * B + s, 1:2, :] = total[:, cols]
-            colsend[i * B + s, 2:3, :] = match[:, cols]
-
-    def col_copy(k):
-        slot = mod(own_at + k, H * B)
-        i, s = div(slot, B), mod(slot, B)
-        to = (half * H + i) * G + s * rep + r
-        return remote(colsend.at[slot], colrecv.at[own_at], col_sent, col_came, to)
-
-    for k in range(1, H * B):
-        col_copy(k).start()
-    colrecv[own_at] = colsend[own_at]
+    peak = jnp.max(col_peak[...], axis=0, keepdims=True)
+    total = jnp.sum(col_total[...] * jnp.exp2(col_peak[...] - peak), axis=0, keepdims=True)
+    match = jnp.sum(col_match[...], axis=0, keepdims=True)
+    for at, di, dv in offsets:
+        for k in range(2):
+            slot = at * 2 + k
+            cols = slice(slot * n, (slot + 1) * n)
+            colsend[slot, 0:1, :] = peak[:, cols]
+            colsend[slot, 1:2, :] = total[:, cols]
+            colsend[slot, 2:3, :] = match[:, cols]
+            if slot:
+                back = group((H - di) % H, (V - dv) % V) * 2 + k
+                remote(
+                    colsend.at[slot], colrecv.at[back], col_sent, col_came,
+                    image_member(di, dv, k),
+                ).start()
+    colrecv[0] = colsend[0]
 
     def joined(parts, count):
         peak = parts[0, 0:1, :]
@@ -502,7 +520,7 @@
     U, V = grid_of(blk, rep)
     N = blk * rep
     H, B = U // 2, V * 2
-    C = B * n
+    C = H * B * n
     f32, i32 = jnp.float32, jnp.int32
     _, _, image_sems, caption_sems = semaphore_counts(U, V, rep)
     dma = lambda count: pltpu.SemaphoreType.DMA((count,))
@@ -519,16 +537,16 @@
             pltpu.VMEM((H * B, n, width), images.dtype),
             pltpu.VMEM((2, 1, n), i32),
             pltpu.VMEM((N, 1, n), i32),
-            pltpu.VMEM((H, 1, C), f32),
-            pltpu.VMEM((H, 1, C), i32),
+            pltpu.VMEM((1, C), f32),
+            pltpu.VMEM((1, C), i32),
             pltpu.VMEM((2 * rep, n, LANES), i32),
             pltpu.VMEM((2 * rep, n, LANES), f32),
             pltpu.VMEM((2 * rep, n, LANES), f32),
             pltpu.VMEM((2 * rep, n, LANES), f32),
             pltpu.VMEM((2 * rep, n, LANES), f32),
-            pltpu.VMEM((H, SUBLANES, C), f32),
-            pltpu.VMEM((H, SUBLANES, C), f32),
-            pltpu.VMEM((H, SUBLANES, C), f32),
+            pltpu.VMEM((SUBLANES, C), f32),
+            pltpu.VMEM((SUBLANES, C), f32),
+            pltpu.VMEM((SUBLANES, C), f32),
             pltpu.VMEM((2 * rep, 8, n), f32),
             pltpu.VMEM((2 * rep, 8, n), f32),
             pltpu.VMEM((H * B, 8, n), f32),

time: 35.9 us -> 35.7 us (level)
  no operation moved by 1% of the time
where the time goes in v4:
time: 35.7 us; the launch traced here: 35.5 us
  Pallas kernels  34.9 us (98%)
  between operations  0.64 us (2%)
    pallas_call x1, Pallas kernels, local(): pl.pallas_call(functools.partial(kernel, blk, rep), out_shape=pltpu.VMEM(...  34.3 us

profile of v4, /device:TPU:0, one launch (start us, length us, event | category | flops | bytes accessed | tf_op | source)
XLA Modules:
  0.0 35.5 jit_solution(10402214199248621519)
XLA Ops:
  0.6 34.3 %shard_map.67.terms_ref = f32[8,192]{1,0:T(8,128)S(1)} custom-call(bf16[192,768]{1,0:T(8,128)(2,1)} %cap_ref.1, bf16[192,768]{1,0:T(8,128)(2,1)} %img_ref.1, s32[1,192]{1,0:T(1,128)} %bitcast.5, s32[1,192]{1,0:T(1,128)} %bitcast.6), custom_call_target="tpu_custom_call" | custom-call | tf_op jit(solution)/shard_map/pallas_call | solution.py:529
  35.0 0.6 %shard_map.68 = (f32[1,192]{1,0:T(1,128)}, f32[1,192]{1,0:T(1,128)}, f32[1,1]{1,0:T(1,128)}) custom-call(f32[8,192]{1,0:T(8,128)S(1)} %shard_map.67.terms_ref), custom_call_target="tpu_custom_call" | custom-call | tf_op jit(solution)/shard_map/pallas_call | solution.py:559

commit v5 on v4

--- a/solution.py
+++ b/solution.py
@@ -65,7 +65,7 @@
     H = U // 2
     B = V * 2
     n, width = cap_ref.shape
-    early = (V + H - 1) * 2 * n
+    early = V + H - 1
     C = H * B * n
     along_sems, across_sems, _, _ = semaphore_counts(U, V, rep)
     b, r = lax.axis_index("blk"), lax.axis_index("rep")
@@ -261,11 +261,13 @@
     for k in range(CAPTION_PIECES - CAPTIONS_HELD, CAPTION_PIECES):
         own_captions_across(k)
 
-    pieces = [((k + 1) / IMAGE_PIECES, 0, k) for k in range(IMAGE_PIECES)]
-    pieces += [((k + 1) / CAPTION_PIECES, 1, k) for k in range(CAPTION_PIECES)]
-    pieces.sort()
-    for _, is_caption, k in pieces:
-        if is_caption:
+    def arrivals(lag):
+        order = [((k + 1) / CAPTION_PIECES, False, k) for k in range(CAPTION_PIECES)]
+        order += [((k + 1) / IMAGE_PIECES + lag, True, k) for k in range(IMAGE_PIECES)]
+        return sorted(order)
+
+    for _, is_image, k in arrivals(0):
+        if not is_image:
             @pl.when(jnp.logical_not(keeps_own))
             def _():
                 relay_captions(0, k)
@@ -310,7 +312,7 @@
     low = aim - start.astype(jnp.int32)
     depth = lax.broadcasted_iota(jnp.int32, picked.shape, 0)
     ok = jnp.sum(jnp.where(depth == low, picked, 0.0), axis=0, keepdims=True)
-    own_ok = ok[:, 2 * rep * n :]
+    own_ok = ok[:, 2 * rep * n :] > 0
     for s in range(2 * rep):
         ok_row = ok[:, s * n : (s + 1) * n]
         bias = to_column(jnp.where(ok_row > 0, 0.0, very_low))
@@ -331,44 +333,46 @@
         return y
 
     def tally(s, cols, scores, first, rows):
-        scaled = scores * log2_e
-        bias, ids = image_bias[:, cols], image_ids[:, cols]
+        scaled = scores * log2_e + image_bias[:, cols]
+        ids = image_ids[:, cols]
         old_peak = col_peak[:, cols]
         peak, match = old_peak, col_match[:, cols]
         wide = lambda x: jnp.concatenate([x] * (scores.shape[1] // LANES), axis=1)
-        peaks = []
+        held, peaks = [], []
         for q in range(rows // SUBLANES):
             at = pl.ds(first + q * SUBLANES, SUBLANES)
-            x = scaled[q * SUBLANES : (q + 1) * SUBLANES]
-            peaks.append(jnp.maximum(fold(x + bias, jnp.maximum), row_peak[s, at]))
-            peak = jnp.maximum(peak, x + wide(caption_bias[s, at]))
+            x = scaled[q * SUBLANES : (q + 1) * SUBLANES] + wide(caption_bias[s, at])
+            held.append(x)
+            peaks.append(jnp.maximum(fold(x, jnp.maximum), row_peak[s, at]))
+            peak = jnp.maximum(peak, x)
             picked = jnp.where(wide(target[s, at]) == ids, x, 0.0)
             row_match[s, at] = row_match[s, at] + fold(picked, jnp.add)
             match = match + picked
         total = col_total[:, cols] * jnp.exp2(old_peak - peak)
         for q in range(rows // SUBLANES):
             at = pl.ds(first + q * SUBLANES, SUBLANES)
-            x = scaled[q * SUBLANES : (q + 1) * SUBLANES]
-            powers = jnp.exp2(x + bias - wide(peaks[q]))
+            powers = jnp.exp2(held[q] - wide(peaks[q]))
             row_total[s, at] = row_total[s, at] * jnp.exp2(row_peak[s, at] - peaks[q]) + fold(
                 powers, jnp.add
             )
             row_peak[s, at] = peaks[q]
-            total = total + jnp.exp2(x + wide(caption_bias[s, at]) - peak)
+            total = total + jnp.exp2(held[q] - peak)
         col_peak[:, cols] = peak
         col_total[:, cols] = total
         col_match[:, cols] = match
 
     def score(s, count, start, stop, first, rows):
         left = caps[pl.ds(s, count), pl.ds(first, rows)].reshape(count * rows, width)
-        right = imgs[start // n : stop // n].reshape(stop - start, width)
-        scores = lax.dot_general(
-            left, right, (((1,), (1,)), ((), ())), preferred_element_type=jnp.float32
-        )
-        for k in range(count):
-            tally(s + k, slice(start, stop), scores[k * rows : (k + 1) * rows], first, rows)
-
-    for at in range(early // (2 * n)):
+        for at in range(start, stop):
+            scores = lax.dot_general(
+                left, imgs[2 * at : 2 * at + 2].reshape(2 * n, width), (((1,), (1,)), ((), ())),
+                preferred_element_type=jnp.float32,
+            )
+            cols = slice(2 * at * n, 2 * (at + 1) * n)
+            for k in range(count):
+                tally(s + k, cols, scores[k * rows : (k + 1) * rows], first, rows)
+
+    for at in range(early):
         beside_came(at)
 
     @pl.loop(0, rep + 1)
@@ -376,10 +380,10 @@
         for step in range(rep + 1):
             @pl.when(e == step)
             def _():
-                for share, is_caption, k in pieces:
-                    if min(rep, 1 + math.ceil(share * rep - 1) if k else is_caption ^ 1) != step:
+                for share, is_image, k in arrivals(1 / IMAGE_PIECES):
+                    if min(rep, math.ceil(share * CAPTION_PIECES) - 1) != step:
                         continue
-                    if is_caption:
+                    if not is_image:
                         relay_captions(1, k)
                     else:
                         for di in range(1, H):
@@ -392,10 +396,9 @@
             came(caps.at[0], cap_recv.at[2 * CAPTION_PIECES + e - 1])
         score(e, 1, 0, early, 0, n)
 
-    for at in range(early // (2 * n), H * V):
+    for at in range(early, H * V):
         beside_came(at)
-    if early < C:
-        score(0, rep + 1, early, C, 0, n)
+    score(0, rep + 1, early, H * V, 0, n)
 
     def row_copy(s):
         away, d = div(s, rep), mod(s, rep)
@@ -421,8 +424,7 @@
         def _():
             rowrecv[half * rep + r] = rowsend[s]
 
-    @pl.loop(0, rep + 1)
-    def _(s):
+    for s in range(rep + 1):
         send_rows(s)
 
     @pl.loop(1, rep)
@@ -435,7 +437,7 @@
                 cap_recv.at[2 * CAPTION_PIECES + rep - 1 + (d - 1) * LAST_PIECES + k],
             )
 
-            score(rep + d, 1, 0, C, k * rows, rows)
+            score(rep + d, 1, 0, H * V, k * rows, rows)
         send_rows(rep + d)
 
     peak = jnp.max(col_peak[...], axis=0, keepdims=True)
@@ -475,10 +477,10 @@
     def _():
         came(rowrecv, row_came)
 
-    caption_loss = own_ok * joined(rowrecv, 2 * rep)
+    caption_loss = jnp.where(own_ok, joined(rowrecv, 2 * rep), 0.0)
     terms_ref[0:1, :] = caption_loss
     came(colrecv.at[pl.ds(0, H * B - 1)], col_came)
-    image_loss = raw[0].astype(jnp.float32) * joined(colrecv, H * B)
+    image_loss = jnp.where(raw[0] > 0, joined(colrecv, H * B), 0.0)
     terms_ref[1:2, :] = image_loss
     own_sum = jnp.sum(caption_loss + image_loss, axis=1, keepdims=True)
     part[me] = jnp.broadcast_to(own_sum, (1, LANES))

time: 35.7 us -> 35.6 us (level)
  no operation moved by 1% of the time
where the time goes in v5:
time: 35.6 us; the launch traced here: 35.4 us
  Pallas kernels  34.8 us (98%)
  between operations  0.64 us (2%)
    pallas_call x1, Pallas kernels, local(): pl.pallas_call(functools.partial(kernel, blk, rep), out_shape=pltpu.VMEM(...  34.2 us

profile of v5, /device:TPU:0, one launch (start us, length us, event | category | flops | bytes accessed | tf_op | source)
XLA Modules:
  0.0 35.4 jit_solution(5564629985791991067)
XLA Ops:
  0.6 34.2 %shard_map.67.terms_ref = f32[8,192]{1,0:T(8,128)S(1)} custom-call(bf16[192,768]{1,0:T(8,128)(2,1)} %cap_ref.1, bf16[192,768]{1,0:T(8,128)(2,1)} %img_ref.1, s32[1,192]{1,0:T(1,128)} %bitcast.5, s32[1,192]{1,0:T(1,128)} %bitcast.6), custom_call_target="tpu_custom_call" | custom-call | tf_op jit(solution)/shard_map/pallas_call | solution.py:531
  34.8 0.6 %shard_map.68 = (f32[1,192]{1,0:T(1,128)}, f32[1,192]{1,0:T(1,128)}, f32[1,1]{1,0:T(1,128)}) custom-call(f32[8,192]{1,0:T(8,128)S(1)} %shard_map.67.terms_ref), custom_call_target="tpu_custom_call" | custom-call | tf_op jit(solution)/shard_map/pallas_call | solution.py:561

commit v6 on v5

--- a/solution.py
+++ b/solution.py
@@ -54,9 +54,9 @@
 
 def kernel(
     blk, rep, cap_ref, img_ref, pos_ref, val_ref, terms_ref,
-    mine, caps, imgs, raw, words, image_bias, image_ids, target, caption_bias,
+    mine, caps, imgs, raw, words, image_bias, image_ids, target, caption_bias, caption_ok,
     row_peak, row_total, row_match, col_peak, col_total, col_match,
-    rowsend, rowrecv, colsend, colrecv, part,
+    rowsend, rowrecv, rowpool, colsend, colrecv, colpool, part, spare,
     loc_sem, img_recv, cap_recv, send_sem, recv_sem,
 ):
     U, V = grid_of(blk, rep)
@@ -76,10 +76,16 @@
     g = mod(me, G)
     half, h = div(u, H), mod(u, H)
     keeps_own = div(u, 2) == h
-    img_sent, cap_sent, line_sent, plane_sent, row_sent, col_sent, part_sent = (
-        send_sem.at[k] for k in range(7)
+    img_sent, cap_sent, line_sent, plane_sent, row_sent, col_sent, row_given, col_given, part_sent = (
+        send_sem.at[k] for k in range(9)
     )
-    line_came, plane_came, row_came, col_came, part_came = (recv_sem.at[k] for k in range(5))
+    line_came, plane_came, row_came, col_came, row_pooled, col_pooled, part_came = (
+        recv_sem.at[k] for k in range(7)
+    )
+    pools = (c == 1) & ((u == H - 1) | (u == H))
+
+    def pool_of(uu, vv, rr):
+        return member(H - 1 + div(uu, H), vv, 1, rr)
 
     def near_of(uu):
         return jnp.where(uu > 2 * mod(uu, H), 1, 0)
@@ -299,7 +305,7 @@
         uu = 2 * h + jnp.where(away == 0, near, 1 - near)
         return ((v * 2 + c) * rep + mod(r + d, rep)) * U + uu
 
-    aims = [words[seat_row(s)] >> 1 for s in range(2 * rep)] + [words[g * U + u] >> 1]
+    aims = [words[seat_row(s)] >> 1 for s in range(2 * rep)]
     aim = jnp.concatenate(aims, axis=1)
     order = lax.broadcasted_iota(jnp.int32, (N, aim.shape[1]), 0)
     starts = (mod(order, U) * G + div(order, U)) * n
@@ -312,9 +318,9 @@
     low = aim - start.astype(jnp.int32)
     depth = lax.broadcasted_iota(jnp.int32, picked.shape, 0)
     ok = jnp.sum(jnp.where(depth == low, picked, 0.0), axis=0, keepdims=True)
-    own_ok = ok[:, 2 * rep * n :] > 0
     for s in range(2 * rep):
         ok_row = ok[:, s * n : (s + 1) * n]
+        caption_ok[s] = ok_row
         bias = to_column(jnp.where(ok_row > 0, 0.0, very_low))
         caption_bias[s] = jnp.broadcast_to(bias, (n, LANES))
         aim_column = to_column(aims[s].astype(jnp.float32)).astype(jnp.int32)
@@ -400,29 +406,37 @@
         beside_came(at)
     score(0, rep + 1, early, H * V, 0, n)
 
-    def row_copy(s):
+    stride = pl.cdiv(n, LANES) * LANES
+
+    def pack(ref, at, ok, first, peak, total, match):
+        ref[at, :, 0:n] = jnp.where(ok, peak, 0.0)
+        ref[at, :, stride : stride + n] = jnp.where(ok, total, jnp.where(first, 1.0, 0.0))
+        ref[at, :, 2 * stride : 2 * stride + n] = jnp.where(ok, match, 0.0)
+
+    def send_rows(s):
         away, d = div(s, rep), mod(s, rep)
         uu = 2 * h + jnp.where(away == 0, near, 1 - near)
+        rr = mod(r + d, rep)
         at = half * rep + r
-        return remote(
-            rowsend.at[s], rowrecv.at[at], row_sent, row_came, member(uu, v, c, mod(r + d, rep))
-        )
-
-    def send_rows(s):
         peak = jnp.max(row_peak[s], axis=1, keepdims=True)
         total = jnp.sum(row_total[s] * jnp.exp2(row_peak[s] - peak), axis=1, keepdims=True)
-        rowsend[s, 0:1, :] = to_row(peak)
-        rowsend[s, 1:2, :] = to_row(total)
-        rowsend[s, 2:3, :] = to_row(jnp.sum(row_match[s], axis=1, keepdims=True))
+        match = jnp.sum(row_match[s], axis=1, keepdims=True)
+        pack(rowsend, s, caption_ok[s] > 0, at == 0, to_row(peak), to_row(total), to_row(match))
+        remote(
+            rowsend.at[s], rowpool.at[(mod(uu, H) * 2 + c) * 2 * rep + at], row_given, row_pooled,
+            pool_of(uu, v, rr),
+        ).start()
         stays = keeps_own & (s == 0)
 
         @pl.when(jnp.logical_not(stays))
         def _():
-            row_copy(s).start()
+            remote(
+                rowsend.at[s], rowrecv.at[at], row_sent, row_came, member(uu, v, c, rr)
+            ).start()
 
         @pl.when(stays)
         def _():
-            rowrecv[half * rep + r] = rowsend[s]
+            rowrecv[at] = rowsend[s]
 
     for s in range(rep + 1):
         send_rows(s)
@@ -447,9 +461,35 @@
         for k in range(2):
             slot = at * 2 + k
             cols = slice(slot * n, (slot + 1) * n)
-            colsend[slot, 0:1, :] = peak[:, cols]
-            colsend[slot, 1:2, :] = total[:, cols]
-            colsend[slot, 2:3, :] = match[:, cols]
+            back = group((H - di) % H, (V - dv) % V) * 2 + k
+            pack(
+                colsend, slot, image_bias[:, cols] == 0, back == 0, peak[:, cols], total[:, cols],
+                match[:, cols],
+            )
+    for at, di, dv in reversed(offsets):
+        for k in range(2):
+            slot = at * 2 + k
+            back = group((H - di) % H, (V - dv) % V) * 2 + k
+            cc = c if k == 0 else 1 - c
+            seat = (mod(h + di, H) * 2 + cc) * H * B + back
+
+            def give():
+                remote(
+                    colsend.at[slot], colpool.at[seat], col_given, col_pooled,
+                    pool_of(u, mod(v + dv, V), r),
+                ).start()
+
+            if dv:
+                give()
+            else:
+                @pl.when(pools)
+                def _():
+                    colpool[seat] = colsend[slot]
+
+                pl.when(jnp.logical_not(pools))(give)
+    for at, di, dv in reversed(offsets):
+        for k in range(2):
+            slot = at * 2 + k
             if slot:
                 back = group((H - di) % H, (V - dv) % V) * 2 + k
                 remote(
@@ -458,17 +498,41 @@
                 ).start()
     colrecv[0] = colsend[0]
 
-    def joined(parts, count):
-        peak = parts[0, 0:1, :]
+    def joined(parts, first, count):
+        piece = lambda s, k: parts[first + s, :, k * stride : k * stride + n]
+        peak = piece(0, 0)
         for s in range(1, count):
-            peak = jnp.maximum(peak, parts[s, 0:1, :])
+            peak = jnp.maximum(peak, piece(s, 0))
         total = jnp.zeros_like(peak)
         match = jnp.zeros_like(peak)
         for s in range(count):
-            total += parts[s, 1:2, :] * jnp.exp2(parts[s, 0:1, :] - peak)
-            match += parts[s, 2:3, :]
+            total += piece(s, 1) * jnp.exp2(piece(s, 0) - peak)
+            match += piece(s, 2)
         return (peak - match) * ln_2 + jnp.log(total)
 
+    pool_count = 2 * V * rep
+    own_pool = (half * V + v) * rep + r
+
+    @pl.when(pools)
+    def _():
+        came(rowpool, row_pooled)
+        whole = jnp.zeros((1, n), jnp.float32)
+        for k in range(2 * H):
+            whole += joined(rowpool, k * 2 * rep, 2 * rep)
+        came(colpool.at[pl.ds(0, 2 * H * (H * B - 1))], col_pooled)
+        for k in range(2 * H):
+            whole += joined(colpool, k * H * B, H * B)
+        part[own_pool] = jnp.broadcast_to(jnp.sum(whole, axis=1, keepdims=True), (1, LANES))
+
+        @pl.loop(0, N)
+        def _(k):
+            uu = div(k, G)
+            to = jnp.where(u < H, U - 1 - uu, uu) * G + mod(k, G)
+
+            @pl.when(to != me)
+            def _():
+                remote(part.at[own_pool], part.at[own_pool], part_sent, part_came, to).start()
+
     @pl.when(keeps_own)
     def _():
         came(rowrecv.at[pl.ds(0, 2 * rep - 1)], row_came)
@@ -477,17 +541,9 @@
     def _():
         came(rowrecv, row_came)
 
-    caption_loss = jnp.where(own_ok, joined(rowrecv, 2 * rep), 0.0)
-    terms_ref[0:1, :] = caption_loss
+    terms_ref[0:1, :] = joined(rowrecv, 0, 2 * rep)
     came(colrecv.at[pl.ds(0, H * B - 1)], col_came)
-    image_loss = jnp.where(raw[0] > 0, joined(colrecv, H * B), 0.0)
-    terms_ref[1:2, :] = image_loss
-    own_sum = jnp.sum(caption_loss + image_loss, axis=1, keepdims=True)
-    part[me] = jnp.broadcast_to(own_sum, (1, LANES))
-
-    @pl.loop(1, N)
-    def _(k):
-        remote(part.at[me], part.at[me], part_sent, part_came, mod(me + k, N)).start()
+    terms_ref[1:2, :] = joined(colrecv, 0, H * B)
 
     sent(words.at[pl.ds(0, U - 1)], line_sent)
     sent(words.at[pl.ds(0, (G - 1) * U)], plane_sent)
@@ -503,9 +559,19 @@
         sent(caps, cap_sent)
         sent(rowsend, row_sent)
 
+    sent(rowsend, row_given)
     sent(colsend.at[pl.ds(0, H * B - 1)], col_sent)
-    sent(part.at[pl.ds(0, N - 1)], part_sent)
-    came(part.at[pl.ds(0, N - 1)], part_came)
+
+    @pl.when(pools)
+    def _():
+        sent(colsend.at[pl.ds(0, H * B - 2 * H)], col_given)
+        sent(spare.at[pl.ds(0, N - 1)], part_sent)
+        came(part.at[pl.ds(0, pool_count - 1)], part_came)
+
+    @pl.when(jnp.logical_not(pools))
+    def _():
+        sent(colsend, col_given)
+        came(part, part_came)
 
     whole = jnp.sum(part[:, 0, :], axis=0, keepdims=True)
     terms_ref[2:3, 0:1] = whole[:, 0:1] / (2.0 * image_total)
@@ -523,6 +589,7 @@
     N = blk * rep
     H, B = U // 2, V * 2
     C = H * B * n
+    packed = 3 * pl.cdiv(n, LANES) * LANES
     f32, i32 = jnp.float32, jnp.int32
     _, _, image_sems, caption_sems = semaphore_counts(U, V, rep)
     dma = lambda count: pltpu.SemaphoreType.DMA((count,))
@@ -543,18 +610,22 @@
             pltpu.VMEM((1, C), i32),
             pltpu.VMEM((2 * rep, n, LANES), i32),
             pltpu.VMEM((2 * rep, n, LANES), f32),
+            pltpu.VMEM((2 * rep, 1, n), f32),
             pltpu.VMEM((2 * rep, n, LANES), f32),
             pltpu.VMEM((2 * rep, n, LANES), f32),
             pltpu.VMEM((2 * rep, n, LANES), f32),
             pltpu.VMEM((SUBLANES, C), f32),
             pltpu.VMEM((SUBLANES, C), f32),
             pltpu.VMEM((SUBLANES, C), f32),
-            pltpu.VMEM((2 * rep, 8, n), f32),
-            pltpu.VMEM((2 * rep, 8, n), f32),
-            pltpu.VMEM((H * B, 8, n), f32),
-            pltpu.VMEM((H * B, 8, n), f32),
+            pltpu.VMEM((2 * rep, 1, packed), f32),
+            pltpu.VMEM((2 * rep, 1, packed), f32),
+            pltpu.VMEM((2 * H * 2 * rep, 1, packed), f32),
+            pltpu.VMEM((H * B, 1, packed), f32),
+            pltpu.VMEM((H * B, 1, packed), f32),
+            pltpu.VMEM((2 * H * H * B, 1, packed), f32),
+            pltpu.VMEM((2 * V * rep, 1, LANES), f32),
             pltpu.VMEM((N, 1, LANES), f32),
-            dma(5), dma(image_sems), dma(caption_sems), dma(7), dma(5),
+            dma(5), dma(image_sems), dma(caption_sems), dma(9), dma(7),
         ],
         compiler_params=pltpu.CompilerParams(collective_id=0, has_side_effects=True),
     )(captions, images, positives.reshape(1, n), valid.reshape(1, n))

time: 35.6 us -> 33.8 us (0.949)
  Pallas kernels: 34.8 us -> 33 us
    pallas_call x1, Pallas kernels: 34.2 us -> 32.4 us  [local(): pl.pallas_call(functools.partial(kernel, blk, rep), out_shape=pltpu.VMEM(...]
where the time goes in v6:
time: 33.8 us; the launch traced here: 33.6 us
  Pallas kernels  33 us (98%)
  between operations  0.64 us (2%)
    pallas_call x1, Pallas kernels, local(): pl.pallas_call(functools.partial(kernel, blk, rep), out_shape=pltpu.VMEM(...  32.4 us

profile of v6, /device:TPU:0, one launch (start us, length us, event | category | flops | bytes accessed | tf_op | source)
XLA Modules:
  0.0 33.6 jit_solution(10586937025306056257)
XLA Ops:
  0.6 32.4 %shard_map.67.terms_ref = f32[8,192]{1,0:T(8,128)S(1)} custom-call(bf16[192,768]{1,0:T(8,128)(2,1)} %cap_ref.1, bf16[192,768]{1,0:T(8,128)(2,1)} %img_ref.1, s32[1,192]{1,0:T(1,128)} %bitcast.5, s32[1,192]{1,0:T(1,128)} %bitcast.6), custom_call_target="tpu_custom_call" | custom-call | tf_op jit(solution)/shard_map/pallas_call | solution.py:598
  33.1 0.6 %shard_map.68 = (f32[1,192]{1,0:T(1,128)}, f32[1,192]{1,0:T(1,128)}, f32[1,1]{1,0:T(1,128)}) custom-call(f32[8,192]{1,0:T(8,128)S(1)} %shard_map.67.terms_ref), custom_call_target="tpu_custom_call" | custom-call | tf_op jit(solution)/shard_map/pallas_call | solution.py:632

commit v7 on v6

--- a/solution.py
+++ b/solution.py
@@ -15,6 +15,8 @@
 LAST_PIECES = 2
 IMAGES_HELD = 1
 CAPTIONS_HELD = 2
+FAR_FIRST = 2
+LATE_LAST = 2
 LANES = 128
 SUBLANES = 8
 log2_e = math.log2(math.e)
@@ -130,9 +132,9 @@
     load_img = pltpu.make_async_copy(img_ref, imgs.at[0], loc_sem.at[2])
     load_cap = pltpu.make_async_copy(cap_ref, mine, loc_sem.at[3])
     keep_cap = pltpu.make_async_copy(cap_ref, caps.at[0], loc_sem.at[4])
+    load_img.start()
     load_val.start()
     load_pos.start()
-    load_img.start()
     load_cap.start()
 
     @pl.when(keeps_own)
@@ -143,11 +145,6 @@
     load_pos.wait()
     words[g * U + u] = raw[1] * 2 + raw[0]
     load_img.wait()
-    load_cap.wait()
-
-    @pl.when(keeps_own)
-    def _():
-        keep_cap.wait()
 
     pl.semaphore_wait(barrier, len(others))
 
@@ -196,7 +193,7 @@
             cap_recv.at[away * CAPTION_PIECES + k], member(to, v, c, r),
         )
 
-    def cap_across(away, d, k):
+    def cap_across(away, d, k, block=None):
         rows = caption_rows(k)
         seat = rep - d
         sem = 2 * CAPTION_PIECES + seat - 1
@@ -204,7 +201,8 @@
             piece = k // (CAPTION_PIECES // LAST_PIECES)
             sem = 2 * CAPTION_PIECES + rep - 1 + (seat - 1) * LAST_PIECES + piece
         return remote(
-            caps.at[away * rep, rows], caps.at[away * rep + seat, rows], cap_sent,
+            (caps.at[away * rep] if block is None else block).at[rows],
+            caps.at[away * rep + seat, rows], cap_sent,
             cap_recv.at[sem], member(u, v, c, mod(r + d, rep)),
         )
 
@@ -229,7 +227,7 @@
         @pl.when(keeps_own)
         def _():
             for d in range(1, rep):
-                cap_across(0, d, k).start()
+                cap_across(0, d, k, mine).start()
 
     for k in range(1, U):
         line_copy(k).start()
@@ -239,6 +237,7 @@
         if k < IMAGE_PIECES - IMAGES_HELD:
             own_across(k)
         img_beside(0, 0, k).start()
+    load_cap.wait()
     for k in range(CAPTION_PIECES):
         for t in range(2):
             @pl.when(t * H + div(u, 2) != u)
@@ -267,25 +266,36 @@
     for k in range(CAPTION_PIECES - CAPTIONS_HELD, CAPTION_PIECES):
         own_captions_across(k)
 
-    def arrivals(lag):
-        order = [((k + 1) / CAPTION_PIECES, False, k) for k in range(CAPTION_PIECES)]
-        order += [((k + 1) / IMAGE_PIECES + lag, True, k) for k in range(IMAGE_PIECES)]
-        return sorted(order)
-
-    for _, is_image, k in arrivals(0):
-        if not is_image:
-            @pl.when(jnp.logical_not(keeps_own))
-            def _():
-                relay_captions(0, k)
-        else:
-            for di in range(1, H):
-                along_came(di, k)
-                for d in range(1, V):
-                    img_across(di, d, k).start()
-                img_beside(di, 0, k).start()
+    def relay_along(k):
+        for di in range(1, H):
+            along_came(di, k)
+            for d in range(1, V):
+                img_across(di, d, k).start()
+            img_beside(di, 0, k).start()
+
+    def relay_own(k):
+        for dv in range(1, V):
+            across_came(0, dv, k)
+            img_beside(0, dv, k).start()
+
+    def relay_late(k):
+        for di in range(1, H):
             for dv in range(1, V):
-                across_came(0, dv, k)
-                img_beside(0, dv, k).start()
+                across_came(di, dv, k)
+                img_beside(di, dv, k).start()
+
+    def relay_near(k):
+        @pl.when(jnp.logical_not(keeps_own))
+        def _():
+            relay_captions(0, k)
+
+    relay_far = functools.partial(relay_captions, 1)
+    relays = [((k + 1) / IMAGE_PIECES, 0, relay_along, k) for k in range(IMAGE_PIECES)]
+    relays += [((k + 1) / IMAGE_PIECES + 0.12, 1, relay_own, k) for k in range(IMAGE_PIECES)]
+    relays += [((k + 1) / CAPTION_PIECES, 2, relay_near, k) for k in range(CAPTION_PIECES)]
+    relays += [(1.02 + k / CAPTION_PIECES, 3, relay_far, k) for k in range(FAR_FIRST)]
+    for _, _, relay, k in sorted(relays, key=lambda x: x[:2]):
+        relay(k)
 
     came(words.at[pl.ds(0, (G - 1) * U)], plane_came)
 
@@ -378,6 +388,10 @@
             for k in range(count):
                 tally(s + k, cols, scores[k * rows : (k + 1) * rows], first, rows)
 
+    @pl.when(keeps_own)
+    def _():
+        keep_cap.wait()
+
     for at in range(early):
         beside_came(at)
 
@@ -386,21 +400,36 @@
         for step in range(rep + 1):
             @pl.when(e == step)
             def _():
-                for share, is_image, k in arrivals(1 / IMAGE_PIECES):
-                    if min(rep, math.ceil(share * CAPTION_PIECES) - 1) != step:
-                        continue
-                    if not is_image:
-                        relay_captions(1, k)
-                    else:
-                        for di in range(1, H):
-                            for dv in range(1, V):
-                                across_came(di, dv, k)
-                                img_beside(di, dv, k).start()
+                for k in range(FAR_FIRST, CAPTION_PIECES):
+                    if step == min(k - FAR_FIRST, rep):
+                        relay_far(k)
+                        late = k - FAR_FIRST - 1
+                        if 0 <= late < IMAGE_PIECES - LATE_LAST:
+                            relay_late(late)
 
         @pl.when((e > 0) & (e < rep))
         def _():
             came(caps.at[0], cap_recv.at[2 * CAPTION_PIECES + e - 1])
         score(e, 1, 0, early, 0, n)
+
+    for k in range(min(CAPTION_PIECES - FAR_FIRST - 1, IMAGE_PIECES - LATE_LAST), IMAGE_PIECES):
+        relay_late(k)
+
+    def last_came(d, k):
+        came(
+            caps.at[rep + d, pl.ds(0, n // LAST_PIECES)],
+            cap_recv.at[2 * CAPTION_PIECES + rep - 1 + (d - 1) * LAST_PIECES + k],
+        )
+
+    def last_early(k):
+        @pl.loop(1, rep)
+        def _(d):
+            last_came(d, k)
+            score(rep + d, 1, 0, early, k * (n // LAST_PIECES), n // LAST_PIECES)
+
+    @pl.loop(0, LAST_PIECES - 1)
+    def _(k):
+        last_early(k)
 
     for at in range(early, H * V):
         beside_came(at)
@@ -441,17 +470,11 @@
     for s in range(rep + 1):
         send_rows(s)
 
+    last_early(LAST_PIECES - 1)
+
     @pl.loop(1, rep)
     def _(d):
-        @pl.loop(0, LAST_PIECES)
-        def _(k):
-            rows = n // LAST_PIECES
-            came(
-                caps.at[rep + d, pl.ds(0, rows)],
-                cap_recv.at[2 * CAPTION_PIECES + rep - 1 + (d - 1) * LAST_PIECES + k],
-            )
-
-            score(rep + d, 1, 0, H * V, k * rows, rows)
+        score(rep + d, 1, early, H * V, 0, n)
         send_rows(rep + d)
 
     peak = jnp.max(col_peak[...], axis=0, keepdims=True)

time: 33.8 us -> 33.5 us (level)
  no operation moved by 1% of the time
where the time goes in v7:
time: 33.5 us; the launch traced here: 33.4 us
  Pallas kernels  32.7 us (98%)
  between operations  0.64 us (2%)
    pallas_call x1, Pallas kernels, local(): pl.pallas_call(functools.partial(kernel, blk, rep), out_shape=pltpu.VMEM(...  32.2 us

profile of v7, /device:TPU:0, one launch (start us, length us, event | category | flops | bytes accessed | tf_op | source)
XLA Modules:
  0.0 33.4 jit_solution(9512627771117985379)
XLA Ops:
  0.6 32.2 %shard_map.67.terms_ref = f32[8,192]{1,0:T(8,128)S(1)} custom-call(bf16[192,768]{1,0:T(8,128)(2,1)} %cap_ref.1, bf16[192,768]{1,0:T(8,128)(2,1)} %img_ref.1, s32[1,192]{1,0:T(1,128)} %bitcast.5, s32[1,192]{1,0:T(1,128)} %bitcast.6), custom_call_target="tpu_custom_call" | custom-call | tf_op jit(solution)/shard_map/pallas_call | solution.py:621
  32.8 0.6 %shard_map.68 = (f32[1,192]{1,0:T(1,128)}, f32[1,192]{1,0:T(1,128)}, f32[1,1]{1,0:T(1,128)}) custom-call(f32[8,192]{1,0:T(8,128)S(1)} %shard_map.67.terms_ref), custom_call_target="tpu_custom_call" | custom-call | tf_op jit(solution)/shard_map/pallas_call | solution.py:655

commit v8 on v7

--- a/solution.py
+++ b/solution.py
@@ -12,11 +12,9 @@
 floor = -1e29
 IMAGE_PIECES = 4
 CAPTION_PIECES = 6
-LAST_PIECES = 2
 IMAGES_HELD = 1
 CAPTIONS_HELD = 2
 FAR_FIRST = 2
-LATE_LAST = 2
 LANES = 128
 SUBLANES = 8
 log2_e = math.log2(math.e)
@@ -43,7 +41,7 @@
     H = U // 2
     along = (H - 1) * IMAGE_PIECES
     across = H * (V - 1) * IMAGE_PIECES
-    return along, across, along + across + H * V, 2 * CAPTION_PIECES + (rep - 1) * (1 + LAST_PIECES)
+    return along, across, along + across + H * V, 2 * CAPTION_PIECES + 2 * (rep - 1)
 
 
 def group_at(V, H, di, dv):
@@ -196,10 +194,7 @@
     def cap_across(away, d, k, block=None):
         rows = caption_rows(k)
         seat = rep - d
-        sem = 2 * CAPTION_PIECES + seat - 1
-        if away:
-            piece = k // (CAPTION_PIECES // LAST_PIECES)
-            sem = 2 * CAPTION_PIECES + rep - 1 + (seat - 1) * LAST_PIECES + piece
+        sem = 2 * CAPTION_PIECES + away * (rep - 1) + seat - 1
         return remote(
             (caps.at[away * rep] if block is None else block).at[rows],
             caps.at[away * rep + seat, rows], cap_sent,
@@ -284,16 +279,29 @@
                 across_came(di, dv, k)
                 img_beside(di, dv, k).start()
 
+    def late_pieces(first, stop):
+        for k in range(min(first, IMAGE_PIECES), min(stop, IMAGE_PIECES)):
+            relay_late(k)
+
+    def far_pieces(first, to_end):
+        for k in range(first, CAPTION_PIECES if to_end else min(first + 1, CAPTION_PIECES)):
+            relay_far(k)
+
     def relay_near(k):
         @pl.when(jnp.logical_not(keeps_own))
         def _():
             relay_captions(0, k)
 
-    relay_far = functools.partial(relay_captions, 1)
+    def relay_far(k):
+        relay_captions(1, k)
+
+    def relay_far_early(k):
+        pl.when(keeps_own)(functools.partial(relay_far, k))
+
     relays = [((k + 1) / IMAGE_PIECES, 0, relay_along, k) for k in range(IMAGE_PIECES)]
     relays += [((k + 1) / IMAGE_PIECES + 0.12, 1, relay_own, k) for k in range(IMAGE_PIECES)]
     relays += [((k + 1) / CAPTION_PIECES, 2, relay_near, k) for k in range(CAPTION_PIECES)]
-    relays += [(1.02 + k / CAPTION_PIECES, 3, relay_far, k) for k in range(FAR_FIRST)]
+    relays += [(1.02 + k / CAPTION_PIECES, 3, relay_far_early, k) for k in range(FAR_FIRST)]
     for _, _, relay, k in sorted(relays, key=lambda x: x[:2]):
         relay(k)
 
@@ -392,6 +400,14 @@
     def _():
         keep_cap.wait()
 
+    @pl.when(keeps_own)
+    def _():
+        far_pieces(FAR_FIRST, False)
+
+    @pl.when(jnp.logical_not(keeps_own))
+    def _():
+        far_pieces(0, False)
+
     for at in range(early):
         beside_came(at)
 
@@ -400,37 +416,28 @@
         for step in range(rep + 1):
             @pl.when(e == step)
             def _():
-                for k in range(FAR_FIRST, CAPTION_PIECES):
-                    if step == min(k - FAR_FIRST, rep):
-                        relay_far(k)
-                        late = k - FAR_FIRST - 1
-                        if 0 <= late < IMAGE_PIECES - LATE_LAST:
-                            relay_late(late)
+                @pl.when(keeps_own)
+                def _():
+                    if step:
+                        late_pieces(step - 1, step)
+                    far_pieces(FAR_FIRST + 1 + step, step == rep)
+                    if step == rep:
+                        late_pieces(step, IMAGE_PIECES)
+
+                @pl.when(jnp.logical_not(keeps_own))
+                def _():
+                    far_pieces(1 + step, False)
+                    if step == rep:
+                        late_pieces(0, IMAGE_PIECES // 2)
+                        far_pieces(2 + step, False)
+                        late_pieces(IMAGE_PIECES // 2, IMAGE_PIECES)
+                        far_pieces(3 + step, True)
 
         @pl.when((e > 0) & (e < rep))
         def _():
             came(caps.at[0], cap_recv.at[2 * CAPTION_PIECES + e - 1])
         score(e, 1, 0, early, 0, n)
 
-    for k in range(min(CAPTION_PIECES - FAR_FIRST - 1, IMAGE_PIECES - LATE_LAST), IMAGE_PIECES):
-        relay_late(k)
-
-    def last_came(d, k):
-        came(
-            caps.at[rep + d, pl.ds(0, n // LAST_PIECES)],
-            cap_recv.at[2 * CAPTION_PIECES + rep - 1 + (d - 1) * LAST_PIECES + k],
-        )
-
-    def last_early(k):
-        @pl.loop(1, rep)
-        def _(d):
-            last_came(d, k)
-            score(rep + d, 1, 0, early, k * (n // LAST_PIECES), n // LAST_PIECES)
-
-    @pl.loop(0, LAST_PIECES - 1)
-    def _(k):
-        last_early(k)
-
     for at in range(early, H * V):
         beside_came(at)
     score(0, rep + 1, early, H * V, 0, n)
@@ -442,41 +449,56 @@
         ref[at, :, stride : stride + n] = jnp.where(ok, total, jnp.where(first, 1.0, 0.0))
         ref[at, :, 2 * stride : 2 * stride + n] = jnp.where(ok, match, 0.0)
 
-    def send_rows(s):
-        away, d = div(s, rep), mod(s, rep)
-        uu = 2 * h + jnp.where(away == 0, near, 1 - near)
-        rr = mod(r + d, rep)
-        at = half * rep + r
+    def pack_rows(s):
         peak = jnp.max(row_peak[s], axis=1, keepdims=True)
         total = jnp.sum(row_total[s] * jnp.exp2(row_peak[s] - peak), axis=1, keepdims=True)
         match = jnp.sum(row_match[s], axis=1, keepdims=True)
-        pack(rowsend, s, caption_ok[s] > 0, at == 0, to_row(peak), to_row(total), to_row(match))
-        remote(
-            rowsend.at[s], rowpool.at[(mod(uu, H) * 2 + c) * 2 * rep + at], row_given, row_pooled,
-            pool_of(uu, v, rr),
-        ).start()
-        stays = keeps_own & (s == 0)
-
-        @pl.when(jnp.logical_not(stays))
-        def _():
+        pack(
+            rowsend, s, caption_ok[s] > 0, half * rep + r == 0, to_row(peak), to_row(total),
+            to_row(match),
+        )
+
+    def row_place(s):
+        away, d = s // rep, s % rep
+        uu = 2 * h + (near if away == 0 else 1 - near)
+        return uu, mod(r + d, rep)
+
+    def pool_rows(s):
+        uu, rr = row_place(s)
+        at = (mod(uu, H) * 2 + c) * 2 * rep + half * rep + r
+        remote(rowsend.at[s], rowpool.at[at], row_given, row_pooled, pool_of(uu, v, rr)).start()
+
+    def send_rows(s):
+        uu, rr = row_place(s)
+        at = half * rep + r
+
+        def go():
             remote(
                 rowsend.at[s], rowrecv.at[at], row_sent, row_came, member(uu, v, c, rr)
             ).start()
 
-        @pl.when(stays)
-        def _():
-            rowrecv[at] = rowsend[s]
+        if s:
+            go()
+        else:
+            pl.when(jnp.logical_not(keeps_own))(go)
+
+            @pl.when(keeps_own)
+            def _():
+                rowrecv[at] = rowsend[s]
 
     for s in range(rep + 1):
+        pack_rows(s)
+    for s in range(rep + 1):
+        pool_rows(s)
         send_rows(s)
-
-    last_early(LAST_PIECES - 1)
 
     @pl.loop(1, rep)
     def _(d):
-        score(rep + d, 1, early, H * V, 0, n)
-        send_rows(rep + d)
-
+        came(caps.at[rep + d], cap_recv.at[2 * CAPTION_PIECES + rep - 1 + d - 1])
+        score(rep + d, 1, 0, H * V, 0, n)
+
+    for s in range(rep + 1, 2 * rep):
+        pack_rows(s)
     peak = jnp.max(col_peak[...], axis=0, keepdims=True)
     total = jnp.sum(col_total[...] * jnp.exp2(col_peak[...] - peak), axis=0, keepdims=True)
     match = jnp.sum(col_match[...], axis=0, keepdims=True)
@@ -489,6 +511,8 @@
                 colsend, slot, image_bias[:, cols] == 0, back == 0, peak[:, cols], total[:, cols],
                 match[:, cols],
             )
+    for s in range(rep + 1, 2 * rep):
+        pool_rows(s)
     for at, di, dv in reversed(offsets):
         for k in range(2):
             slot = at * 2 + k
@@ -510,6 +534,8 @@
                     colpool[seat] = colsend[slot]
 
                 pl.when(jnp.logical_not(pools))(give)
+    for s in range(rep + 1, 2 * rep):
+        send_rows(s)
     for at, di, dv in reversed(offsets):
         for k in range(2):
             slot = at * 2 + k

time: 33.5 us -> 33.4 us (level)
  no operation moved by 1% of the time
where the time goes in v8:
time: 33.4 us; the launch traced here: 33.2 us
  Pallas kernels  32.6 us (98%)
  between operations  0.64 us (2%)
    pallas_call x1, Pallas kernels, local(): pl.pallas_call(functools.partial(kernel, blk, rep), out_shape=pltpu.VMEM(...  32 us

profile of v8, /device:TPU:0, one launch (start us, length us, event | category | flops | bytes accessed | tf_op | source)
XLA Modules:
  0.0 33.2 jit_solution(3091087534491369894)
XLA Ops:
  0.6 32.0 %shard_map.67.terms_ref = f32[8,192]{1,0:T(8,128)S(1)} custom-call(bf16[192,768]{1,0:T(8,128)(2,1)} %cap_ref.1, bf16[192,768]{1,0:T(8,128)(2,1)} %img_ref.1, s32[1,192]{1,0:T(1,128)} %bitcast.5, s32[1,192]{1,0:T(1,128)} %bitcast.6), custom_call_target="tpu_custom_call" | custom-call | tf_op jit(solution)/shard_map/pallas_call | solution.py:647
  32.7 0.6 %shard_map.68 = (f32[1,192]{1,0:T(1,128)}, f32[1,192]{1,0:T(1,128)}, f32[1,1]{1,0:T(1,128)}) custom-call(f32[8,192]{1,0:T(8,128)S(1)} %shard_map.67.terms_ref), custom_call_target="tpu_custom_call" | custom-call | tf_op jit(solution)/shard_map/pallas_call | solution.py:681

commit v9 on v8

--- a/solution.py
+++ b/solution.py
@@ -253,6 +253,45 @@
     row_total[...] = jnp.zeros(row_total.shape, jnp.float32)
     row_match[...] = jnp.zeros(row_match.shape, jnp.float32)
 
+    def relay_along(k):
+        for di in range(1, H):
+            along_came(di, k)
+            for d in range(1, V):
+                img_across(di, d, k).start()
+            img_beside(di, 0, k).start()
+
+    def relay_own(k):
+        for dv in range(1, V):
+            across_came(0, dv, k)
+            img_beside(0, dv, k).start()
+
+    def relay_late(k):
+        for di in range(1, H):
+            for dv in range(1, V):
+                across_came(di, dv, k)
+                img_beside(di, dv, k).start()
+
+    def late_pieces(first, stop):
+        for k in range(min(first, IMAGE_PIECES), min(stop, IMAGE_PIECES)):
+            relay_late(k)
+
+    def far_pieces(first, stop):
+        for k in range(first, stop):
+            relay_far(k)
+
+    def relay_near(k):
+        @pl.when(jnp.logical_not(keeps_own))
+        def _():
+            relay_captions(0, k)
+
+    def relay_far(k):
+        relay_captions(1, k)
+
+    def relay_far_early(k):
+        pl.when(keeps_own)(functools.partial(relay_far, k))
+
+    relay_near(0)
+
     came(words.at[pl.ds(0, U - 1)], line_came)
     for k in range(1, G):
         plane_copy(k).start()
@@ -261,46 +300,9 @@
     for k in range(CAPTION_PIECES - CAPTIONS_HELD, CAPTION_PIECES):
         own_captions_across(k)
 
-    def relay_along(k):
-        for di in range(1, H):
-            along_came(di, k)
-            for d in range(1, V):
-                img_across(di, d, k).start()
-            img_beside(di, 0, k).start()
-
-    def relay_own(k):
-        for dv in range(1, V):
-            across_came(0, dv, k)
-            img_beside(0, dv, k).start()
-
-    def relay_late(k):
-        for di in range(1, H):
-            for dv in range(1, V):
-                across_came(di, dv, k)
-                img_beside(di, dv, k).start()
-
-    def late_pieces(first, stop):
-        for k in range(min(first, IMAGE_PIECES), min(stop, IMAGE_PIECES)):
-            relay_late(k)
-
-    def far_pieces(first, to_end):
-        for k in range(first, CAPTION_PIECES if to_end else min(first + 1, CAPTION_PIECES)):
-            relay_far(k)
-
-    def relay_near(k):
-        @pl.when(jnp.logical_not(keeps_own))
-        def _():
-            relay_captions(0, k)
-
-    def relay_far(k):
-        relay_captions(1, k)
-
-    def relay_far_early(k):
-        pl.when(keeps_own)(functools.partial(relay_far, k))
-
     relays = [((k + 1) / IMAGE_PIECES, 0, relay_along, k) for k in range(IMAGE_PIECES)]
     relays += [((k + 1) / IMAGE_PIECES + 0.12, 1, relay_own, k) for k in range(IMAGE_PIECES)]
-    relays += [((k + 1) / CAPTION_PIECES, 2, relay_near, k) for k in range(CAPTION_PIECES)]
+    relays += [((k + 1) / CAPTION_PIECES, 2, relay_near, k) for k in range(1, CAPTION_PIECES)]
     relays += [(1.02 + k / CAPTION_PIECES, 3, relay_far_early, k) for k in range(FAR_FIRST)]
     for _, _, relay, k in sorted(relays, key=lambda x: x[:2]):
         relay(k)
@@ -402,47 +404,67 @@
 
     @pl.when(keeps_own)
     def _():
-        far_pieces(FAR_FIRST, False)
+        far_pieces(FAR_FIRST, FAR_FIRST + 1)
 
     @pl.when(jnp.logical_not(keeps_own))
     def _():
-        far_pieces(0, False)
+        far_pieces(0, 1)
 
     for at in range(early):
         beside_came(at)
 
-    @pl.loop(0, rep + 1)
+    @pl.loop(0, rep)
     def _(e):
-        for step in range(rep + 1):
+        for step in range(rep):
             @pl.when(e == step)
             def _():
                 @pl.when(keeps_own)
                 def _():
                     if step:
                         late_pieces(step - 1, step)
-                    far_pieces(FAR_FIRST + 1 + step, step == rep)
-                    if step == rep:
-                        late_pieces(step, IMAGE_PIECES)
+                    far_pieces(FAR_FIRST + 1 + step, FAR_FIRST + 2 + step)
 
                 @pl.when(jnp.logical_not(keeps_own))
                 def _():
-                    far_pieces(1 + step, False)
-                    if step == rep:
-                        late_pieces(0, IMAGE_PIECES // 2)
-                        far_pieces(2 + step, False)
-                        late_pieces(IMAGE_PIECES // 2, IMAGE_PIECES)
-                        far_pieces(3 + step, True)
-
-        @pl.when((e > 0) & (e < rep))
+                    far_pieces(1 + step, 2 + step)
+
+        @pl.when(e > 0)
         def _():
             came(caps.at[0], cap_recv.at[2 * CAPTION_PIECES + e - 1])
         score(e, 1, 0, early, 0, n)
 
+    @pl.when(keeps_own)
+    def _():
+        late_pieces(rep - 1, rep)
+        far_pieces(FAR_FIRST + 1 + rep, CAPTION_PIECES)
+
+    @pl.when(jnp.logical_not(keeps_own))
+    def _():
+        far_pieces(1 + rep, CAPTION_PIECES - 2)
+
+    upper = n // CAPTION_PIECES * (CAPTION_PIECES - 2)
+    score(rep, 1, 0, early, 0, upper)
+
+    @pl.when(keeps_own)
+    def _():
+        late_pieces(rep, IMAGE_PIECES)
+
+    @pl.when(jnp.logical_not(keeps_own))
+    def _():
+        late_pieces(0, IMAGE_PIECES - 2)
+        far_pieces(CAPTION_PIECES - 2, CAPTION_PIECES - 1)
+        late_pieces(IMAGE_PIECES - 2, IMAGE_PIECES)
+        far_pieces(CAPTION_PIECES - 1, CAPTION_PIECES)
+
+    score(rep, 1, 0, early, upper, n - upper)
+
     for at in range(early, H * V):
         beside_came(at)
     score(0, rep + 1, early, H * V, 0, n)
 
     stride = pl.cdiv(n, LANES) * LANES
+
+    sums = slice(0, 2 * stride)
 
     def pack(ref, at, ok, first, peak, total, match):
         ref[at, :, 0:n] = jnp.where(ok, peak, 0.0)
@@ -466,7 +488,10 @@
     def pool_rows(s):
         uu, rr = row_place(s)
         at = (mod(uu, H) * 2 + c) * 2 * rep + half * rep + r
-        remote(rowsend.at[s], rowpool.at[at], row_given, row_pooled, pool_of(uu, v, rr)).start()
+        remote(
+            rowsend.at[s], rowpool.at[at], row_given, row_pooled,
+            pool_of(uu, v, mod(rr + 1, rep)),
+        ).start()
 
     def send_rows(s):
         uu, rr = row_place(s)
@@ -522,7 +547,7 @@
 
             def give():
                 remote(
-                    colsend.at[slot], colpool.at[seat], col_given, col_pooled,
+                    colsend.at[slot, :, sums], colpool.at[seat], col_given, col_pooled,
                     pool_of(u, mod(v + dv, V), r),
                 ).start()
 
@@ -531,7 +556,7 @@
             else:
                 @pl.when(pools)
                 def _():
-                    colpool[seat] = colsend[slot]
+                    colpool[seat] = colsend[slot, :, sums]
 
                 pl.when(jnp.logical_not(pools))(give)
     for s in range(rep + 1, 2 * rep):
@@ -547,7 +572,7 @@
                 ).start()
     colrecv[0] = colsend[0]
 
-    def joined(parts, first, count):
+    def joined(parts, first, count, matches=1):
         piece = lambda s, k: parts[first + s, :, k * stride : k * stride + n]
         peak = piece(0, 0)
         for s in range(1, count):
@@ -556,8 +581,9 @@
         match = jnp.zeros_like(peak)
         for s in range(count):
             total += piece(s, 1) * jnp.exp2(piece(s, 0) - peak)
-            match += piece(s, 2)
-        return (peak - match) * ln_2 + jnp.log(total)
+            if matches:
+                match += piece(s, 2)
+        return (peak - matches * match) * ln_2 + jnp.log(total)
 
     pool_count = 2 * V * rep
     own_pool = (half * V + v) * rep + r
@@ -567,10 +593,10 @@
         came(rowpool, row_pooled)
         whole = jnp.zeros((1, n), jnp.float32)
         for k in range(2 * H):
-            whole += joined(rowpool, k * 2 * rep, 2 * rep)
+            whole += joined(rowpool, k * 2 * rep, 2 * rep, 2)
         came(colpool.at[pl.ds(0, 2 * H * (H * B - 1))], col_pooled)
         for k in range(2 * H):
-            whole += joined(colpool, k * H * B, H * B)
+            whole += joined(colpool, k * H * B, H * B, 0)
         part[own_pool] = jnp.broadcast_to(jnp.sum(whole, axis=1, keepdims=True), (1, LANES))
 
         @pl.loop(0, N)
@@ -613,13 +639,13 @@
 
     @pl.when(pools)
     def _():
-        sent(colsend.at[pl.ds(0, H * B - 2 * H)], col_given)
+        sent(colsend.at[pl.ds(0, H * B - 2 * H), :, sums], col_given)
         sent(spare.at[pl.ds(0, N - 1)], part_sent)
         came(part.at[pl.ds(0, pool_count - 1)], part_came)
 
     @pl.when(jnp.logical_not(pools))
     def _():
-        sent(colsend, col_given)
+        sent(colsend.at[:, :, sums], col_given)
         came(part, part_came)
 
     whole = jnp.sum(part[:, 0, :], axis=0, keepdims=True)
@@ -671,7 +697,7 @@
             pltpu.VMEM((2 * H * 2 * rep, 1, packed), f32),
             pltpu.VMEM((H * B, 1, packed), f32),
             pltpu.VMEM((H * B, 1, packed), f32),
-            pltpu.VMEM((2 * H * H * B, 1, packed), f32),
+            pltpu.VMEM((2 * H * H * B, 1, packed // 3 * 2), f32),
             pltpu.VMEM((2 * V * rep, 1, LANES), f32),
             pltpu.VMEM((N, 1, LANES), f32),
             dma(5), dma(image_sems), dma(caption_sems), dma(9), dma(7),

time: 33.4 us -> 33 us (0.988)
  no operation moved by 1% of the time
where the time goes in v9:
time: 33 us; the launch traced here: 32.9 us
  Pallas kernels  32.3 us (98%)
  between operations  0.64 us (2%)
    pallas_call x1, Pallas kernels, local(): pl.pallas_call(functools.partial(kernel, blk, rep), out_shape=pltpu.VMEM(...  31.7 us

profile of v9, /device:TPU:0, one launch (start us, length us, event | category | flops | bytes accessed | tf_op | source)
XLA Modules:
  0.0 32.9 jit_solution(9211023362945741095)
XLA Ops:
  0.6 31.7 %shard_map.67.terms_ref = f32[8,192]{1,0:T(8,128)S(1)} custom-call(bf16[192,768]{1,0:T(8,128)(2,1)} %cap_ref.1, bf16[192,768]{1,0:T(8,128)(2,1)} %img_ref.1, s32[1,192]{1,0:T(1,128)} %bitcast.5, s32[1,192]{1,0:T(1,128)} %bitcast.6), custom_call_target="tpu_custom_call" | custom-call | tf_op jit(solution)/shard_map/pallas_call | solution.py:673
  32.3 0.6 %shard_map.68 = (f32[1,192]{1,0:T(1,128)}, f32[1,192]{1,0:T(1,128)}, f32[1,1]{1,0:T(1,128)}) custom-call(f32[8,192]{1,0:T(8,128)S(1)} %shard_map.67.terms_ref), custom_call_target="tpu_custom_call" | custom-call | tf_op jit(solution)/shard_map/pallas_call | solution.py:707

commit v10 on v9

--- a/solution.py
+++ b/solution.py
@@ -10,7 +10,7 @@
 
 very_low = -1e30
 floor = -1e29
-IMAGE_PIECES = 4
+IMAGE_PIECES = 3
 CAPTION_PIECES = 6
 IMAGES_HELD = 1
 CAPTIONS_HELD = 2
@@ -76,8 +76,8 @@
     g = mod(me, G)
     half, h = div(u, H), mod(u, H)
     keeps_own = div(u, 2) == h
-    img_sent, cap_sent, line_sent, plane_sent, row_sent, col_sent, row_given, col_given, part_sent = (
-        send_sem.at[k] for k in range(9)
+    img_sent, cap_sent, words_sent, row_sent, col_sent, col_given, part_sent = (
+        send_sem.at[k] for k in range(7)
     )
     line_came, plane_came, row_came, col_came, row_pooled, col_pooled, part_came = (
         recv_sem.at[k] for k in range(7)
@@ -208,11 +208,11 @@
 
     def line_copy(k):
         row = words.at[g * U + u]
-        return remote(row, row, line_sent, line_came, mod(u + k, U) * G + g)
+        return remote(row, row, words_sent, line_came, mod(u + k, U) * G + g)
 
     def plane_copy(k):
         rows = words.at[pl.ds(g * U, U)]
-        return remote(rows, rows, plane_sent, plane_came, u * G + mod(g + k, G))
+        return remote(rows, rows, words_sent, plane_came, u * G + mod(g + k, G))
 
     def own_across(k):
         for d in range(1, V):
@@ -489,7 +489,7 @@
         uu, rr = row_place(s)
         at = (mod(uu, H) * 2 + c) * 2 * rep + half * rep + r
         remote(
-            rowsend.at[s], rowpool.at[at], row_given, row_pooled,
+            rowsend.at[s], rowpool.at[at], row_sent, row_pooled,
             pool_of(uu, v, mod(rr + 1, rep)),
         ).start()
 
@@ -599,7 +599,7 @@
             whole += joined(colpool, k * H * B, H * B, 0)
         part[own_pool] = jnp.broadcast_to(jnp.sum(whole, axis=1, keepdims=True), (1, LANES))
 
-        @pl.loop(0, N)
+        @pl.loop(0, N, unroll=4)
         def _(k):
             uu = div(k, G)
             to = jnp.where(u < H, U - 1 - uu, uu) * G + mod(k, G)
@@ -620,21 +620,19 @@
     came(colrecv.at[pl.ds(0, H * B - 1)], col_came)
     terms_ref[1:2, :] = joined(colrecv, 0, H * B)
 
-    sent(words.at[pl.ds(0, U - 1)], line_sent)
-    sent(words.at[pl.ds(0, (G - 1) * U)], plane_sent)
+    sent(words.at[pl.ds(0, N - 1)], words_sent)
     sent(imgs.at[pl.ds(0, H * B - 1)], img_sent)
 
     @pl.when(keeps_own)
     def _():
         sent(caps.at[pl.ds(0, 2 * rep - 1)], cap_sent)
-        sent(rowsend.at[pl.ds(0, 2 * rep - 1)], row_sent)
+        sent(rowpool.at[pl.ds(0, 4 * rep - 1)], row_sent)
 
     @pl.when(jnp.logical_not(keeps_own))
     def _():
         sent(caps, cap_sent)
-        sent(rowsend, row_sent)
-
-    sent(rowsend, row_given)
+        sent(rowpool.at[pl.ds(0, 4 * rep)], row_sent)
+
     sent(colsend.at[pl.ds(0, H * B - 1)], col_sent)
 
     @pl.when(pools)
@@ -700,7 +698,7 @@
             pltpu.VMEM((2 * H * H * B, 1, packed // 3 * 2), f32),
             pltpu.VMEM((2 * V * rep, 1, LANES), f32),
             pltpu.VMEM((N, 1, LANES), f32),
-            dma(5), dma(image_sems), dma(caption_sems), dma(9), dma(7),
+            dma(5), dma(image_sems), dma(caption_sems), dma(7), dma(7),
         ],
         compiler_params=pltpu.CompilerParams(collective_id=0, has_side_effects=True),
     )(captions, images, positives.reshape(1, n), valid.reshape(1, n))

time: 33 us -> 32.9 us (level)
  no operation moved by 1% of the time
where the time goes in v10:
time: 32.9 us; the launch traced here: 32.7 us
  Pallas kernels  32.1 us (98%)
  between operations  0.64 us (2%)
    pallas_call x1, Pallas kernels, local(): pl.pallas_call(functools.partial(kernel, blk, rep), out_shape=pltpu.VMEM(...  31.5 us

profile of v10, /device:TPU:0, one launch (start us, length us, event | category | flops | bytes accessed | tf_op | source)
XLA Modules:
  0.0 32.7 jit_solution(4402496055069274744)
XLA Ops:
  0.6 31.5 %shard_map.67.terms_ref = f32[8,192]{1,0:T(8,128)S(1)} custom-call(bf16[192,768]{1,0:T(8,128)(2,1)} %cap_ref.1, bf16[192,768]{1,0:T(8,128)(2,1)} %img_ref.1, s32[1,192]{1,0:T(1,128)} %bitcast.5, s32[1,192]{1,0:T(1,128)} %bitcast.6), custom_call_target="tpu_custom_call" | custom-call | tf_op jit(solution)/shard_map/pallas_call | solution.py:671
  32.2 0.6 %shard_map.68 = (f32[1,192]{1,0:T(1,128)}, f32[1,192]{1,0:T(1,128)}, f32[1,1]{1,0:T(1,128)}) custom-call(f32[8,192]{1,0:T(8,128)S(1)} %shard_map.67.terms_ref), custom_call_target="tpu_custom_call" | custom-call | tf_op jit(solution)/shard_map/pallas_call | solution.py:705
